TPU v7x, 32 devices: a whole 2x2x4 slice. The times are simulated.
32 devices in a mesh: term: 4 (over y, x), sector: 8 (over z, core).
Axes of the slice: x: 2, y: 2, z: 4, core: 2. Of those that a mesh axis runs over, the one named last changes fastest.
Arguments:
- wavefunction: float32 [8, 512, 512], P('sector'), may hold values from -120 to 120
- precond: float32 [8, 512, 512], P('sector', 'term'), may hold values from 0.05 to 4
- left_ops: float32 [8, 16, 512, 512], P('sector', 'term'), may hold values from -0.5 to 4.5
- right_ops: float32 [8, 16, 512, 512], P('sector', 'term'), may hold values from -1 to 2
- out_sector: int32 [8, 16], P('sector', 'term'), may hold values from 0 to 7, as said below
- live_counts: int32 [8, 4], P('sector', 'term'), may hold values from 1 to 4, as said below
Outputs:
- first_image: float32 [8, 512, 512], P('sector', 'term')
- correction: float32 [8, 512, 512], P('sector', 'term')
- second_image: float32 [8, 512, 512], P('sector', 'term')
Inputs may be any that keep to these rules, and one draw needn't show every extreme that they name: Each term moves the charge by at most one sector: out_sector[s, j] differs from s by at most 1. `live_counts`: in every sector some device has all 4 slots live.
All inputs are finite; a program needn't handle non-finite values.
Results may differ from a plain program's by a relative error of at most 0.0003.
Values sent between devices are 32-bit elements; how exact they have to be, the bound alone decides.
A program may use at most 64 MiB of HBM per device.

v0:
```python
import functools

import jax
import jax.numpy as jnp
from jax import lax
from jax.experimental import pallas as pl
from jax.experimental.pallas import tpu as pltpu
from jax.sharding import PartitionSpec as P

F32 = jnp.float32
MESH = pl.DeviceIdType.MESH
VMEM = pl.BlockSpec(memory_space=pltpu.VMEM)


def split(x):
    high = x.astype(jnp.bfloat16)
    return high, (x - high.astype(F32)).astype(jnp.bfloat16)


def product(a_high, a_low, b_high, b_low):
    dot = functools.partial(jnp.dot, preferred_element_type=F32)
    return dot(a_high, b_high) + dot(a_high, b_low) + dot(a_low, b_high)


def terms_kernel(target, count, v_ref, left_ref, right_ref, out_ref, v_high, v_low, r_high, r_low):
    slot = pl.program_id(0)
    width = v_ref.shape[0]
    piece = min(256, width)

    @pl.when(slot == 0)
    def _():
        out_ref[...] = jnp.zeros_like(out_ref)
        v_high[...], v_low[...] = split(v_ref[...])

    @pl.when(slot < count[0, 0])
    def _():
        place = target[0, slot] - lax.axis_index("sector") + 1
        r_high[...], r_low[...] = split(right_ref[...])
        for start in range(0, width, piece):
            rows = pl.ds(start, piece)
            left_high, left_low = split(left_ref[rows])
            inner = product(left_high, left_low, v_high[...], v_low[...])
            in_high, in_low = split(inner)
            out_ref[place, rows] += product(in_high, in_low, r_high[...], r_low[...])


def all_terms(vector, left_ops, right_ops, out_sector, live_counts):
    slots, width = left_ops.shape[1], left_ops.shape[2]

    def live(j, target, count):
        return (0, jnp.minimum(j, count[0, 0] - 1), 0, 0)

    return pl.pallas_call(
        terms_kernel,
        out_shape=jax.ShapeDtypeStruct((3, width, width), F32),
        grid_spec=pltpu.PrefetchScalarGridSpec(
            num_scalar_prefetch=2,
            grid=(slots,),
            in_specs=[
                pl.BlockSpec((width, width), lambda j, a, b: (0, 0)),
                pl.BlockSpec((None, None, width, width), live),
                pl.BlockSpec((None, None, width, width), live),
            ],
            out_specs=pl.BlockSpec((3, width, width), lambda j, a, b: (0, 0, 0)),
            scratch_shapes=[pltpu.VMEM((width, width), jnp.bfloat16)] * 4,
        ),
        compiler_params=pltpu.CompilerParams(dimension_semantics=("arbitrary",), vmem_limit_bytes=40 << 20),
    )(out_sector, live_counts, vector, left_ops, right_ops)


def send(source, target, send_sem, recv_sem, **where):
    return pltpu.make_async_remote_copy(
        src_ref=source, dst_ref=target, send_sem=send_sem, recv_sem=recv_sem,
        device_id=where, device_id_type=MESH,
    )


def greet():
    terms, sectors = lax.axis_size("term"), lax.axis_size("sector")
    t, s = lax.axis_index("term"), lax.axis_index("sector")
    barrier = pltpu.get_barrier_semaphore()
    for k in range(1, terms):
        pl.semaphore_signal(barrier, inc=1, device_id={"term": lax.rem(t + k, terms)}, device_id_type=MESH)
    for k in range(1, sectors):
        pl.semaphore_signal(barrier, inc=1, device_id={"sector": lax.rem(s + k, sectors)}, device_id_type=MESH)
    pl.semaphore_wait(barrier, terms + sectors - 2)


def exchange(whole, image, bufs):
    up_in, down_in, acc, rs_in, up_s, up_r, down_s, down_r, rs_s, rs_r = bufs
    terms, sectors = lax.axis_size("term"), lax.axis_size("sector")
    t, s = lax.axis_index("term"), lax.axis_index("sector")
    rows = whole.shape[1] // terms

    def slab(r):
        return pl.ds(pl.multiple_of(r * rows, rows), rows)

    def upward(r):
        return send(whole.at[2, slab(r)], up_in.at[slab(r)], up_s.at[r], up_r.at[r], sector=lax.rem(s + 1, sectors))

    def downward(r):
        return send(whole.at[0, slab(r)], down_in.at[slab(r)], down_s.at[r], down_r.at[r],
                    sector=lax.rem(s + sectors - 1, sectors))

    def scatter(r, source):
        return send(acc.at[slab(r)], rs_in.at[source], rs_s.at[r], rs_r.at[source], term=r)

    @pl.loop(0, terms)
    def _(k):
        r = lax.rem(t + 1 + k, terms)

        @pl.when(s + 1 < sectors)
        def _():
            upward(r).start()

        @pl.when(s > 0)
        def _():
            downward(r).start()

    @pl.loop(0, terms)
    def _(k):
        r = lax.rem(t + 1 + k, terms)
        acc[slab(r)] = whole[1, slab(r)]

        @pl.when(s > 0)
        def _():
            upward(r).wait_recv()
            acc[slab(r)] += up_in[slab(r)]

        @pl.when(s + 1 < sectors)
        def _():
            downward(r).wait_recv()
            acc[slab(r)] += down_in[slab(r)]

        @pl.when(k < terms - 1)
        def _():
            scatter(r, t).start()

    image[...] = acc[slab(t)]

    @pl.loop(0, terms - 1)
    def _(k):
        j = lax.rem(t + terms - 1 - k, terms)
        scatter(j, j).wait_recv()
        image[...] += rs_in[j]

    def finish():
        @pl.loop(0, terms)
        def _(k):
            r = lax.rem(t + 1 + k, terms)

            @pl.when(s + 1 < sectors)
            def _():
                upward(r).wait_send()

            @pl.when(s > 0)
            def _():
                downward(r).wait_send()

            @pl.when(k < terms - 1)
            def _():
                scatter(r, t).wait_send()

    return finish


def exchange_scratch(width, terms):
    rows = width // terms
    return [pltpu.VMEM((width, width), F32)] * 3 + [pltpu.VMEM((terms, rows, width), F32)] + [
        pltpu.SemaphoreType.DMA((terms,))
    ] * 6


def first_kernel(whole, wave, precond, image, correction, full, *scratch):
    bufs, (gather, own, mid, term_in, sector_in, ag_s, ag_r, ts_s, ts_r, ss_s, ss_r) = scratch[:10], scratch[10:]
    terms, sectors = lax.axis_size("term"), lax.axis_size("sector")
    t, s = lax.axis_index("term"), lax.axis_index("sector")
    rows = image.shape[0]
    greet()
    finish = exchange(whole, image, bufs)

    w = wave[pl.ds(pl.multiple_of(t * rows, rows), rows)]
    f = image[...]
    p = precond[...]
    wf, ww = w * f, w * w

    def lanes(x):
        line = jnp.sum(x, axis=0, keepdims=True)
        return sum(line[:, c : c + 128] for c in range(0, line.shape[1], 128))

    own[...] = jnp.zeros_like(own)
    for i, x in enumerate((wf, ww, wf * p, ww * p)):
        own[i : i + 1] = lanes(x)

    def to_term(k):
        return send(own, term_in.at[k - 1], ts_s.at[k - 1], ts_r.at[k - 1], term=lax.rem(t + k, terms))

    def to_sector(k):
        return send(mid, sector_in.at[k - 1], ss_s.at[k - 1], ss_r.at[k - 1], sector=lax.rem(s + k, sectors))

    for k in range(1, terms):
        to_term(k).start()
    total = own[...]
    for k in range(1, terms):
        to_term(k).wait_recv()
        total += term_in[k - 1]
    mid[...] = total
    for k in range(1, sectors):
        to_sector(k).start()
    for k in range(1, sectors):
        to_sector(k).wait_recv()
        total += sector_in[k - 1]
    cross, norm, a, b = (jnp.sum(total[i : i + 1], axis=1, keepdims=True) for i in range(4))
    rayleigh = cross / norm
    share = (a - rayleigh * b) / norm
    gather[t] = p * (f - rayleigh * w) - share * w

    def spread(r, source):
        return send(gather.at[source], gather.at[source], ag_s.at[r], ag_r.at[source], term=r)

    for k in range(1, terms):
        spread(lax.rem(t + k, terms), t).start()
    correction[...] = gather[t]
    full[pl.ds(pl.multiple_of(t * rows, rows), rows)] = gather[t]
    for k in range(1, terms):
        j = lax.rem(t + terms - k, terms)
        spread(j, j).wait_recv()
        full[pl.ds(pl.multiple_of(j * rows, rows), rows)] = gather[j]
    finish()
    for k in range(1, terms):
        spread(lax.rem(t + k, terms), t).wait_send()
        to_term(k).wait_send()
    for k in range(1, sectors):
        to_sector(k).wait_send()


def second_kernel(whole, image, *scratch):
    greet()
    exchange(whole, image, scratch)()


def per_device(wavefunction, precond, left_ops, right_ops, out_sector, live_counts):
    terms, sectors = lax.axis_size("term"), lax.axis_size("sector")
    width = wavefunction.shape[1]
    rows = width // terms
    center = wavefunction[0]
    slab = jax.ShapeDtypeStruct((rows, width), F32)
    whole = all_terms(center, left_ops, right_ops, out_sector, live_counts)
    tile = pltpu.VMEM((8, 128), F32)
    dma = pltpu.SemaphoreType.DMA
    first_image, correction, full = pl.pallas_call(
        first_kernel,
        out_shape=(slab, slab, jax.ShapeDtypeStruct((width, width), F32)),
        in_specs=[VMEM] * 3,
        out_specs=(VMEM,) * 3,
        scratch_shapes=exchange_scratch(width, terms) + [
            pltpu.VMEM((terms, rows, width), F32), tile, tile,
            pltpu.VMEM((terms - 1, 8, 128), F32), pltpu.VMEM((sectors - 1, 8, 128), F32),
            dma((terms,)), dma((terms,)), dma((terms - 1,)), dma((terms - 1,)),
            dma((sectors - 1,)), dma((sectors - 1,)),
        ],
        compiler_params=pltpu.CompilerParams(collective_id=0, has_side_effects=True, vmem_limit_bytes=32 << 20),
    )(whole, center, precond[0])
    whole = all_terms(full, left_ops, right_ops, out_sector, live_counts)
    second_image = pl.pallas_call(
        second_kernel,
        out_shape=slab,
        in_specs=[VMEM],
        out_specs=VMEM,
        scratch_shapes=exchange_scratch(width, terms),
        compiler_params=pltpu.CompilerParams(collective_id=1, has_side_effects=True, vmem_limit_bytes=32 << 20),
    )(whole)
    return (first_image[None], correction[None], second_image[None])


def solution(mesh):
    placed = (
        P("sector", None, None),
        P("sector", "term", None),
        P("sector", "term", None, None),
        P("sector", "term", None, None),
        P("sector", "term"),
        P("sector", "term"),
    )
    return jax.shard_map(
        per_device,
        mesh=mesh,
        in_specs=placed,
        out_specs=(P("sector", "term", None), P("sector", "term", None), P("sector", "term", None)),
        check_vma=False,
    )
```

profile of v0, /device:TPU:10, one launch (start us, length us, event | category | flops | bytes accessed | tf_op | source)
XLA Modules:
  0.0 95.2 jit_solution(3985895696022689056)
XLA Ops:
  1.3 0.0 copy-start
  1.3 2.2 %copy-done = f32[1,4,512,512]{3,2,1,0:T(8,128)S(1)} copy-done((f32[1,4,512,512]{3,2,1,0:T(8,128)S(1)}, f32[1,4,512,512]{3,2,1,0:T(8,128)}, u32[]{:S(2)}) %copy-start) | copy-done | bytes 4194328
  3.5 0.0 copy-start.2
  3.5 2.2 %copy-done.2 = f32[1,4,512,512]{3,2,1,0:T(8,128)S(1)} copy-done((f32[1,4,512,512]{3,2,1,0:T(8,128)S(1)}, f32[1,4,512,512]{3,2,1,0:T(8,128)}, u32[]{:S(2)}) %copy-start.2) | copy-done | bytes 4194328
  5.7 0.0 copy-start.4
  5.7 1.2 %copy-done.4 = f32[1,512,512]{2,1,0:T(8,128)S(1)} copy-done((f32[1,512,512]{2,1,0:T(8,128)S(1)}, f32[1,512,512]{2,1,0:T(8,128)}, u32[]{:S(2)}) %copy-start.4) | copy-done | bytes 1048600
  6.9 0.0 copy-start.7
  6.9 0.7 copy-done.7
  7.5 0.0 copy-start.5
  7.5 0.0 copy-start.6
  7.5 0.0 copy-start.3
  7.5 9.0 %shard_map.85.whole = f32[3,512,512]{2,1,0:T(8,128)S(1)} custom-call(s32[1,4]{1,0:T(1,128)S(1)} %copy-done.7, s32[1,1]{1,0:T(1,128)S(6)} %copy.12.count, f32[512,512]{1,0:T(8,128)S(1)} %bitcast.5, f32[1,4,512,512]{3,2,1,0:T(8,128)S(1)} %copy-done, f32[1,4,512,512]{3,2,1,0:T(8,128)S(1)} %copy-done.2), custom_call_target="tpu_custom_call" | custom-call | tf_op jit(solution)/shard_map/pallas_call | solution.py:53
  16.5 0.0 copy-done.5
  16.6 0.0 copy-done.6
  16.6 0.0 copy-start.1
  16.6 44.0 %shard_map.86 = (f32[128,512]{1,0:T(8,128)S(1)}, f32[128,512]{1,0:T(8,128)S(1)}, f32[512,512]{1,0:T(8,128)S(1)}) custom-call(f32[3,512,512]{2,1,0:T(8,128)S(1)} %shard_map.85.whole, f32[512,512]{1,0:T(8,128)S(1)} %bitcast.6, f32[128,512]{1,0:T(8,128)S(1)} %bitcast.8), custom_call_target="tpu_custom_call" | custom-call | tf_op jit(solution)/shard_map/pallas_call | solution.py:251
  60.6 0.0 copy-done.3
  60.6 0.0 copy-done.1
  60.6 9.0 %shard_map.87.whole = f32[3,512,512]{2,1,0:T(8,128)S(1)} custom-call(s32[1,4]{1,0:T(1,128)S(1)} %copy-done.7, s32[1,1]{1,0:T(1,128)S(6)} %copy.12.count, f32[512,512]{1,0:T(8,128)S(1)} %get-tuple-element.8.v_ref, f32[1,4,512,512]{3,2,1,0:T(8,128)S(1)} %copy-done.1, f32[1,4,512,512]{3,2,1,0:T(8,128)S(1)} %copy-done.3), custom_call_target="tpu_custom_call" | custom-call | tf_op jit(solution)/shard_map/pallas_call | solution.py:53
  69.6 23.5 %shard_map.88 = f32[128,512]{1,0:T(8,128)S(1)} custom-call(f32[3,512,512]{2,1,0:T(8,128)S(1)} %shard_map.87.whole), custom_call_target="tpu_custom_call" | custom-call | tf_op jit(solution)/shard_map/pallas_call | solution.py:265
  93.1 0.7 copy.13
  93.8 0.7 copy.14
  94.5 0.7 copy.15
Async XLA Ops:
  1.3 2.2 %copy-start = (f32[1,4,512,512]{3,2,1,0:T(8,128)S(1)}, f32[1,4,512,512]{3,2,1,0:T(8,128)}, u32[]{:S(2)}) copy-start(f32[1,4,512,512]{3,2,1,0:T(8,128)} %left_ref.3) | copy-start | bytes 12582916
  3.5 2.2 %copy-start.2 = (f32[1,4,512,512]{3,2,1,0:T(8,128)S(1)}, f32[1,4,512,512]{3,2,1,0:T(8,128)}, u32[]{:S(2)}) copy-start(f32[1,4,512,512]{3,2,1,0:T(8,128)} %right_ref.3) | copy-start | bytes 12582916
  5.7 1.2 %copy-start.4 = (f32[1,512,512]{2,1,0:T(8,128)S(1)}, f32[1,512,512]{2,1,0:T(8,128)}, u32[]{:S(2)}) copy-start(f32[1,512,512]{2,1,0:T(8,128)} %param.6) | copy-start | bytes 3145732
  6.9 0.7 copy-start.7
  7.5 9.0 %copy-start.5 = (f32[1,512,512]{2,1,0:T(8,128)S(1)}, f32[1,512,512]{2,1,0:T(8,128)}, u32[]{:S(2)}) copy-start(f32[1,512,512]{2,1,0:T(8,128)} %param.6) | copy-start | bytes 3145732
  7.5 9.0 %copy-start.6 = (f32[1,128,512]{2,1,0:T(8,128)S(1)}, f32[1,128,512]{2,1,0:T(8,128)}, u32[]{:S(2)}) copy-start(f32[1,128,512]{2,1,0:T(8,128)} %param.7) | copy-start | bytes 786436
  7.5 53.0 %copy-start.3 = (f32[1,4,512,512]{3,2,1,0:T(8,128)S(1)}, f32[1,4,512,512]{3,2,1,0:T(8,128)}, u32[]{:S(2)}) copy-start(f32[1,4,512,512]{3,2,1,0:T(8,128)} %right_ref.3) | copy-start | bytes 12582916
  16.6 44.0 %copy-start.1 = (f32[1,4,512,512]{3,2,1,0:T(8,128)S(1)}, f32[1,4,512,512]{3,2,1,0:T(8,128)}, u32[]{:S(2)}) copy-start(f32[1,4,512,512]{3,2,1,0:T(8,128)} %left_ref.3) | copy-start | bytes 12582916
where the time goes:
time: 95.5 us; the launch traced here: 95.2 us
  Pallas kernels  85.4 us (89%)
  local copies, waits for them, and re-layouts  8.38 us (9%)
  between operations  1.36 us (1%)
    pallas_call x1, Pallas kernels, per_device(): pl.pallas_call(first_kernel, out_shape=(slab, slab, jax.ShapeDtypeStruct(...  44 us
    pallas_call x1, Pallas kernels, per_device(): pl.pallas_call(second_kernel, out_shape=slab, in_specs=[VMEM], out_specs=...  23.5 us
    pallas_call x2, Pallas kernels, all_terms(): pl.pallas_call(terms_kernel, out_shape=jax.ShapeDtypeStruct((3, width, wi...  18 us
    unnamed x19, local copies, waits for them, and re-layouts  8.38 us

commit v1 on v0

v1 whole, which is shorter than its diff:
```python
import functools
import math

import jax
import jax.numpy as jnp
from jax import lax
from jax.experimental import pallas as pl
from jax.experimental.pallas import tpu as pltpu
from jax.sharding import PartitionSpec as P

F32, BF16 = jnp.float32, jnp.bfloat16
MESH = pl.DeviceIdType.MESH
VMEM = pl.BlockSpec(memory_space=pltpu.VMEM)
SMEM = pl.BlockSpec(memory_space=pltpu.SMEM)
ANY = pl.BlockSpec(memory_space=pl.ANY)
SLICES = 4


def split(x):
    high = x.astype(BF16)
    return high, (x - high.astype(F32)).astype(BF16)


def product(a_high, a_low, b_high, b_low):
    dot = functools.partial(jnp.dot, preferred_element_type=F32)
    return dot(a_high, b_high) + dot(a_high, b_low) + dot(a_low, b_high)


def send(source, target, send_sem, recv_sem, **where):
    return pltpu.make_async_remote_copy(
        src_ref=source, dst_ref=target, send_sem=send_sem, recv_sem=recv_sem,
        device_id=where, device_id_type=MESH,
    )


def grid_of(terms):
    columns = max(d for d in range(1, math.isqrt(terms) + 1) if terms % d == 0)
    return terms // columns, columns


class Place:
    def __init__(self):
        self.terms, self.sectors = lax.axis_size("term"), lax.axis_size("sector")
        self.t, self.s = lax.axis_index("term"), lax.axis_index("sector")
        self.gy, self.gx = grid_of(self.terms)
        self.y, self.x = self.t // self.gx, lax.rem(self.t, self.gx)

    def at(self, dy, dx):
        return lax.rem(self.y + dy, self.gy) * self.gx + lax.rem(self.x + dx, self.gx)

    def order(self):
        both = [(dy, dx) for dy in range(1, self.gy) for dx in range(1, self.gx)]
        return both + [(dy, 0) for dy in range(1, self.gy)] + [(0, dx) for dx in range(1, self.gx)] + [(0, 0)]


def barrier(here):
    sem = pltpu.get_barrier_semaphore()
    for k in range(1, here.terms):
        pl.semaphore_signal(sem, inc=1, device_id={"term": lax.rem(here.t + k, here.terms)}, device_id_type=MESH)
    for k in range(1, here.sectors):
        pl.semaphore_signal(sem, inc=1, device_id={"sector": lax.rem(here.s + k, here.sectors)}, device_id_type=MESH)
    return lambda: pl.semaphore_wait(sem, here.terms + here.sectors - 2)


class Exchange:
    def __init__(self, here, refs):
        self.here = here
        (self.whole, self.up_in, self.down_in, self.acc, self.da_in, self.db_in, self.x_in, self.y_in,
         self.up_s, self.up_r, self.down_s, self.down_r, self.da_s, self.da_r, self.db_s, self.db_r,
         self.x_s, self.x_r, self.y_s, self.y_r) = refs
        self.rows, self.width = self.acc.shape[1], self.acc.shape[2]
        self.sub, self.half = self.rows // SLICES, self.width // 2

    @staticmethod
    def scratch(width, terms):
        rows, half = width // terms, width // 2
        gy, gx = grid_of(terms)
        dma = pltpu.SemaphoreType.DMA
        whole = pltpu.VMEM((terms, rows, width), F32)
        return [
            pltpu.VMEM((3, terms, rows, width), F32), whole, whole, whole,
            pltpu.VMEM((gy, gx, rows, half), F32), pltpu.VMEM((gy, gx, rows, half), F32),
            pltpu.VMEM((gx, rows, width), F32), pltpu.VMEM((gy, rows, width), F32),
        ] + [dma((SLICES, terms))] * 4 + [dma((SLICES, gy, gx))] * 4 + [dma((SLICES, gx))] * 2 + [dma((SLICES, gy))] * 2

    def part(self, i):
        return pl.ds(pl.multiple_of(i * self.sub, self.sub), self.sub)

    def upward(self, r, i):
        h = self.here
        return send(self.whole.at[2, r, self.part(i)], self.up_in.at[r, self.part(i)], self.up_s.at[i, r],
                    self.up_r.at[i, r], sector=lax.rem(h.s + 1, h.sectors))

    def downward(self, r, i):
        h = self.here
        return send(self.whole.at[0, r, self.part(i)], self.down_in.at[r, self.part(i)], self.down_s.at[i, r],
                    self.down_r.at[i, r], sector=lax.rem(h.s + h.sectors - 1, h.sectors))

    def corner_a(self, dy, dx, i):
        h, part = self.here, self.part(i)
        return send(self.acc.at[h.at(dy, dx), part, : self.half], self.da_in.at[dy, dx, part],
                    self.da_s.at[i, dy, dx], self.da_r.at[i, dy, dx], term=h.at(0, dx))

    def corner_b(self, dy, dx, i):
        h, part = self.here, self.part(i)
        return send(self.acc.at[h.at(dy, dx), part, self.half :], self.db_in.at[dy, dx, part],
                    self.db_s.at[i, dy, dx], self.db_r.at[i, dy, dx], term=h.at(dy, 0))

    def along_x(self, dx, i):
        h, part = self.here, self.part(i)
        return send(self.acc.at[h.at(0, dx), part], self.x_in.at[dx, part], self.x_s.at[i, dx], self.x_r.at[i, dx],
                    term=h.at(0, dx))

    def along_y(self, dy, i):
        h, part = self.here, self.part(i)
        return send(self.acc.at[h.at(dy, 0), part], self.y_in.at[dy, part], self.y_s.at[i, dy], self.y_r.at[i, dy],
                    term=h.at(dy, 0))

    def sectors_out(self, i):
        h = self.here
        for dy, dx in h.order():
            r = h.at(dy, dx)

            @pl.when(h.s + 1 < h.sectors)
            def _():
                self.upward(r, i).start()

            @pl.when(h.s > 0)
            def _():
                self.downward(r, i).start()

    def merge(self, r, i):
        h, part = self.here, self.part(i)
        self.acc[r, part] = self.whole[1, r, part]

        @pl.when(h.s > 0)
        def _():
            self.upward(r, i).wait_recv()
            self.acc[r, part] += self.up_in[r, part]

        @pl.when(h.s + 1 < h.sectors)
        def _():
            self.downward(r, i).wait_recv()
            self.acc[r, part] += self.down_in[r, part]

    def corners(self, i):
        h = self.here
        for dy in range(1, h.gy):
            for dx in range(1, h.gx):
                self.merge(h.at(dy, dx), i)
                self.corner_a(dy, dx, i).start()
                self.corner_b(dy, dx, i).start()

    def sides(self, i):
        h, part = self.here, self.part(i)
        for dy in range(1, h.gy):
            r = h.at(dy, 0)
            self.merge(r, i)
            for dx in range(1, h.gx):
                self.corner_a(dy, dx, i).wait_recv()
                self.acc[r, part, : self.half] += self.da_in[dy, dx, part]
            self.along_y(dy, i).start()
        for dx in range(1, h.gx):
            r = h.at(0, dx)
            self.merge(r, i)
            for dy in range(1, h.gy):
                self.corner_b(dy, dx, i).wait_recv()
                self.acc[r, part, self.half :] += self.db_in[dy, dx, part]
            self.along_x(dx, i).start()

    def own(self, i):
        h, part = self.here, self.part(i)
        self.merge(h.t, i)
        total = self.acc[h.t, part]
        for dy in range(1, h.gy):
            self.along_y(dy, i).wait_recv()
            total += self.y_in[dy, part]
        for dx in range(1, h.gx):
            self.along_x(dx, i).wait_recv()
            total += self.x_in[dx, part]
        return total

    def drain(self):
        h = self.here

        @pl.loop(0, SLICES)
        def _(i):
            for dy, dx in h.order():
                r = h.at(dy, dx)

                @pl.when(h.s + 1 < h.sectors)
                def _():
                    self.upward(r, i).wait_send()

                @pl.when(h.s > 0)
                def _():
                    self.downward(r, i).wait_send()

                if dy and dx:
                    self.corner_a(dy, dx, i).wait_send()
                    self.corner_b(dy, dx, i).wait_send()
                elif dy:
                    self.along_y(dy, i).wait_send()
                elif dx:
                    self.along_x(dx, i).wait_send()


class Gather:
    def __init__(self, here, full, refs, pieces):
        self.here, self.full = here, full
        self.x_s, self.x_r, self.y_s, self.y_r, self.a_s, self.a_r, self.b_s, self.b_r = refs
        self.sub, self.half = full.shape[1] // pieces, full.shape[2] // 2
        self.pieces = pieces

    @staticmethod
    def scratch(terms, pieces):
        gy, gx = grid_of(terms)
        dma = pltpu.SemaphoreType.DMA
        return [dma((pieces, gx))] * 2 + [dma((pieces, gy))] * 2 + [dma((pieces, gy, gx))] * 4

    def part(self, i):
        return pl.ds(pl.multiple_of(i * self.sub, self.sub), self.sub)

    def to_x(self, r, dx, i):
        ref = self.full.at[r, self.part(i)]
        return send(ref, ref, self.x_s.at[i, dx], self.x_r.at[i, dx], term=self.here.at(0, dx))

    def to_y(self, r, dy, i):
        ref = self.full.at[r, self.part(i)]
        return send(ref, ref, self.y_s.at[i, dy], self.y_r.at[i, dy], term=self.here.at(dy, 0))

    def relay_a(self, r, dy, dx, i):
        ref = self.full.at[r, self.part(i), : self.half]
        return send(ref, ref, self.a_s.at[i, dy, dx], self.a_r.at[i, dy, dx], term=self.here.at(0, dx))

    def relay_b(self, r, dy, dx, i):
        ref = self.full.at[r, self.part(i), self.half :]
        return send(ref, ref, self.b_s.at[i, dy, dx], self.b_r.at[i, dy, dx], term=self.here.at(dy, 0))

    def begin(self, i):
        h = self.here
        for dx in range(1, h.gx):
            self.to_x(h.t, dx, i).start()
        for dy in range(1, h.gy):
            self.to_y(h.t, dy, i).start()

    def relay(self, i):
        h = self.here
        for dx in range(1, h.gx):
            r = h.at(0, dx)
            self.to_x(r, h.gx - dx, i).wait_recv()
            for dy in range(1, h.gy):
                self.relay_b(r, dy, dx, i).start()
        for dy in range(1, h.gy):
            r = h.at(dy, 0)
            self.to_y(r, h.gy - dy, i).wait_recv()
            for dx in range(1, h.gx):
                self.relay_a(r, dy, dx, i).start()

    def finish(self, i):
        h = self.here
        for dy in range(1, h.gy):
            for dx in range(1, h.gx):
                self.relay_a(h.at(dy, h.gx - dx), dy, dx, i).wait_recv()
                self.relay_b(h.at(h.gy - dy, dx), dy, dx, i).wait_recv()

    def drain(self):
        h = self.here

        @pl.loop(0, self.pieces)
        def _(i):
            for dx in range(1, h.gx):
                self.to_x(h.t, dx, i).wait_send()
            for dy in range(1, h.gy):
                self.to_y(h.t, dy, i).wait_send()
            for dy in range(1, h.gy):
                for dx in range(1, h.gx):
                    self.relay_a(h.at(dy, 0), dy, dx, i).wait_send()
                    self.relay_b(h.at(0, dx), dy, dx, i).wait_send()


EXCHANGE_REFS, GATHER_REFS = 20, 8


def kernel(target, count, wave_hbm, precond_hbm, left_hbm, right_hbm, first_out, correction_out, second_out, *scratch):
    scratch = list(scratch)

    def take(n):
        refs = scratch[:n]
        del scratch[:n]
        return refs

    here = Place()
    first, second = Exchange(here, take(EXCHANGE_REFS)), Exchange(here, take(EXCHANGE_REFS))
    wave, precond, image, left, right, r_high, r_low, v_high, v_low = take(9)
    p_gather, f_gather = Gather(here, precond, take(GATHER_REFS), 1), Gather(here, image, take(GATHER_REFS), SLICES)
    mine, mid, term_in, sector_in, ts_s, ts_r, ss_s, ss_r, load = take(9)
    terms, sectors, t, s = here.terms, here.sectors, here.t, here.s
    slots, _, rows, width = left.shape
    sub = rows // SLICES

    loads = [pltpu.make_async_copy(precond_hbm, precond.at[t], load.at[0]),
             pltpu.make_async_copy(wave_hbm, wave, load.at[1])]
    for j in range(slots):
        loads.append(pltpu.make_async_copy(right_hbm.at[j], right.at[j], load.at[2 + 2 * j]))
        loads.append(pltpu.make_async_copy(left_hbm.at[j], left.at[j], load.at[3 + 2 * j]))
    arrived = barrier(here)
    for copy in loads:
        copy.start()
    loads[0].wait()
    arrived()
    p_gather.begin(0)
    loads[1].wait()
    for r in range(terms):
        v_high[r * rows : (r + 1) * rows], v_low[r * rows : (r + 1) * rows] = split(wave[r])
    for j in range(slots):
        loads[2 + 2 * j].wait()
        r_high[j], r_low[j] = split(right[j])
    for j in range(slots):
        loads[3 + 2 * j].wait()

    def compute(exchange, i):
        part = pl.ds(pl.multiple_of(i * sub, sub), sub)
        for j in range(slots):
            place = target[0, j] - s + 1
            alive = j < count[0, 0]
            left_high, left_low = split(left[j, :, part, :].reshape(terms * sub, width))
            inner = product(left_high, left_low, v_high[...], v_low[...])
            in_high, in_low = split(inner)
            tile = product(in_high, in_low, r_high[j], r_low[j]).reshape(terms, sub, width)
            for p in range(3):
                chosen = jnp.where(jnp.logical_and(alive, place == p), tile, 0.0)
                if j == 0:
                    exchange.whole[p, :, part, :] = chosen
                else:
                    exchange.whole[p, :, part, :] += chosen

    def apply(exchange, finished, relayed):
        @pl.loop(0, SLICES + 3)
        def _(i):
            @pl.when(i < SLICES)
            def _():
                compute(exchange, i)
                exchange.sectors_out(i)

            @pl.when(jnp.logical_and(i >= 1, i < SLICES + 1))
            def _():
                exchange.corners(i - 1)

            @pl.when(jnp.logical_and(i >= 2, i < SLICES + 2))
            def _():
                exchange.sides(i - 2)

            @pl.when(i >= 3)
            def _():
                finished(i - 3, exchange.own(i - 3))

            relayed(i)

    def first_done(i, total):
        part = first.part(i)
        image[t, part] = total
        first_out[part] = total
        f_gather.begin(i)

    def relays(i):
        @pl.when(i == 2)
        def _():
            p_gather.relay(0)

        @pl.when(i >= 5)
        def _():
            f_gather.relay(i - 5)

    apply(first, first_done, relays)

    w, f, p = wave[t], image[t], precond[t]
    wf, ww = w * f, w * w

    def lanes(x):
        line = jnp.sum(x, axis=0, keepdims=True)
        return sum(line[:, c : c + 128] for c in range(0, line.shape[1], 128))

    mine[...] = jnp.zeros_like(mine)
    for i, x in enumerate((wf, ww, wf * p, ww * p)):
        mine[i : i + 1] = lanes(x)

    def to_term(k):
        return send(mine, term_in.at[k - 1], ts_s.at[k - 1], ts_r.at[k - 1], term=lax.rem(t + k, terms))

    def to_sector(k):
        return send(mid, sector_in.at[k - 1], ss_s.at[k - 1], ss_r.at[k - 1], sector=lax.rem(s + k, sectors))

    for k in range(1, terms):
        to_term(k).start()
    f_gather.relay(2)
    total = mine[...]
    for k in range(1, terms):
        to_term(k).wait_recv()
        total += term_in[k - 1]
    mid[...] = total
    for k in range(1, sectors):
        to_sector(k).start()
    f_gather.relay(3)
    p_gather.finish(0)
    for k in range(1, sectors):
        to_sector(k).wait_recv()
        total += sector_in[k - 1]
    cross, norm, a, b = (jnp.sum(total[i : i + 1], axis=1, keepdims=True) for i in range(4))
    rayleigh = cross / norm
    share = (a - rayleigh * b) / norm
    for i in range(SLICES):
        f_gather.finish(i)

    def corrected(r):
        return precond[r] * (image[r] - rayleigh * wave[r]) - share * wave[r]

    for r in range(terms):
        v_high[r * rows : (r + 1) * rows], v_low[r * rows : (r + 1) * rows] = split(corrected(r))
    correction_out[...] = corrected(t)

    def second_done(i, total):
        second_out[second.part(i)] = total

    apply(second, second_done, lambda i: None)

    first.drain()
    second.drain()
    p_gather.drain()
    f_gather.drain()
    for k in range(1, terms):
        to_term(k).wait_send()
    for k in range(1, sectors):
        to_sector(k).wait_send()


def per_device(wavefunction, precond, left_ops, right_ops, out_sector, live_counts):
    terms, sectors = lax.axis_size("term"), lax.axis_size("sector")
    width, slots = wavefunction.shape[1], left_ops.shape[1]
    rows = width // terms
    dma = pltpu.SemaphoreType.DMA
    slab = jax.ShapeDtypeStruct((rows, width), F32)
    block = pltpu.VMEM((terms, rows, width), F32)
    half = pltpu.VMEM((width, width), BF16)
    operators = pltpu.VMEM((slots, terms, rows, width), F32)
    halves = pltpu.VMEM((slots, width, width), BF16)
    tile = pltpu.VMEM((8, 128), F32)
    outs = pl.pallas_call(
        kernel,
        out_shape=(slab,) * 3,
        in_specs=[SMEM] * 2 + [ANY] * 4,
        out_specs=(VMEM,) * 3,
        scratch_shapes=Exchange.scratch(width, terms) * 2
        + [block, block, block, operators, pltpu.VMEM((slots, width, width), F32), halves, halves, half, half]
        + Gather.scratch(terms, 1) + Gather.scratch(terms, SLICES)
        + [tile, tile, pltpu.VMEM((terms - 1, 8, 128), F32), pltpu.VMEM((sectors - 1, 8, 128), F32),
           dma((terms - 1,)), dma((terms - 1,)), dma((sectors - 1,)), dma((sectors - 1,)), dma((2 + 2 * slots,))],
        compiler_params=pltpu.CompilerParams(collective_id=0, has_side_effects=True, vmem_limit_bytes=60 << 20),
    )(out_sector, live_counts, wavefunction.reshape(terms, rows, width), precond[0],
      left_ops.reshape(slots, terms, rows, width), right_ops[0])
    return tuple(x[None] for x in outs)


def solution(mesh):
    placed = (
        P("sector", None, None),
        P("sector", "term", None),
        P("sector", "term", None, None),
        P("sector", "term", None, None),
        P("sector", "term"),
        P("sector", "term"),
    )
    return jax.shard_map(
        per_device,
        mesh=mesh,
        in_specs=placed,
        out_specs=(P("sector", "term", None), P("sector", "term", None), P("sector", "term", None)),
        check_vma=False,
    )
```

time: 95.5 us -> 71.9 us (0.75)
  the two profiles are of different devices: /device:TPU:10 before, /device:TPU:0 now
where the time goes in v1:
time: 71.9 us; the launch traced here: 71.7 us
  Pallas kernels  65.4 us (91%)
  local copies, waits for them, and re-layouts  5.01 us (7%)
  between operations  1.29 us (2%)
    pallas_call x1, Pallas kernels, per_device(): pl.pallas_call(kernel, out_shape=(slab,) * 3, in_specs=[SMEM] * 2 + [ANY]...  65.4 us
    unnamed x3, local copies, waits for them, and re-layouts  5.01 us

profile of v1, /device:TPU:0, one launch (start us, length us, event | category | flops | bytes accessed | tf_op | source)
XLA Modules:
  0.0 71.7 jit_solution(9338910809921625825)
XLA Ops:
  1.3 65.4 %shard_map.85 = (f32[128,512]{1,0:T(8,128)}, f32[128,512]{1,0:T(8,128)}, f32[128,512]{1,0:T(8,128)}) custom-call(s32[1,4]{1,0:T(1,128)} %target.1, s32[1,1]{1,0:T(1,128)S(6)} %copy.12.count, f32[4,128,512]{2,1,0:T(8,128)} %bitcast.9, f32[128,512]{1,0:T(8,128)} %bitcast.10, f32[4,4,128,512]{3,2,1,0:T(8,128)} %bitcast.7, f32[4,512,512]{2,1,0:T(8,128)} %bitcast.8), custom_call_target="tpu_custom_call" | custom-call | tf_op jit(solution)/shard_map/pallas_call | solution.py:448
  66.7 1.7 %copy.13 = f32[1,128,512]{2,1,0:T(8,128)} copy(f32[1,128,512]{2,1,0:T(8,128)} %bitcast.13) | data formatting | bytes 524288
  68.3 1.7 %copy.14 = f32[1,128,512]{2,1,0:T(8,128)} copy(f32[1,128,512]{2,1,0:T(8,128)} %bitcast.12) | data formatting | bytes 524288
  70.0 1.7 %copy.15 = f32[1,128,512]{2,1,0:T(8,128)} copy(f32[1,128,512]{2,1,0:T(8,128)} %bitcast.11) | data formatting | bytes 524288

commit v2 on v1

--- a/solution.py
+++ b/solution.py
@@ -11,9 +11,9 @@
 F32, BF16 = jnp.float32, jnp.bfloat16
 MESH = pl.DeviceIdType.MESH
 VMEM = pl.BlockSpec(memory_space=pltpu.VMEM)
-SMEM = pl.BlockSpec(memory_space=pltpu.SMEM)
-ANY = pl.BlockSpec(memory_space=pl.ANY)
+HBM = pl.BlockSpec(memory_space=pltpu.HBM)
 SLICES = 4
+VMEM_BYTES = 67043328
 
 
 def split(x):
@@ -44,22 +44,26 @@
         self.t, self.s = lax.axis_index("term"), lax.axis_index("sector")
         self.gy, self.gx = grid_of(self.terms)
         self.y, self.x = self.t // self.gx, lax.rem(self.t, self.gx)
+        self.corners = [(dy, dx) for dy in range(1, self.gy) for dx in range(1, self.gx)]
+        self.sides = [(dy, 0) for dy in range(1, self.gy)] + [(0, dx) for dx in range(1, self.gx)] + [(0, 0)]
 
     def at(self, dy, dx):
         return lax.rem(self.y + dy, self.gy) * self.gx + lax.rem(self.x + dx, self.gx)
 
-    def order(self):
-        both = [(dy, dx) for dy in range(1, self.gy) for dx in range(1, self.gx)]
-        return both + [(dy, 0) for dy in range(1, self.gy)] + [(0, dx) for dx in range(1, self.gx)] + [(0, 0)]
+    def peer(self, k):
+        return {"term": lax.rem(self.t + k // self.sectors, self.terms),
+                "sector": lax.rem(self.s + lax.rem(k, self.sectors), self.sectors)}
 
 
 def barrier(here):
     sem = pltpu.get_barrier_semaphore()
-    for k in range(1, here.terms):
-        pl.semaphore_signal(sem, inc=1, device_id={"term": lax.rem(here.t + k, here.terms)}, device_id_type=MESH)
-    for k in range(1, here.sectors):
-        pl.semaphore_signal(sem, inc=1, device_id={"sector": lax.rem(here.s + k, here.sectors)}, device_id_type=MESH)
-    return lambda: pl.semaphore_wait(sem, here.terms + here.sectors - 2)
+    peers = here.terms * here.sectors - 1
+
+    @pl.loop(1, peers + 1)
+    def _(k):
+        pl.semaphore_signal(sem, inc=1, device_id=here.peer(k), device_id_type=MESH)
+
+    return lambda: pl.semaphore_wait(sem, peers)
 
 
 class Exchange:
@@ -116,9 +120,9 @@
         return send(self.acc.at[h.at(dy, 0), part], self.y_in.at[dy, part], self.y_s.at[i, dy], self.y_r.at[i, dy],
                     term=h.at(dy, 0))
 
-    def sectors_out(self, i):
-        h = self.here
-        for dy, dx in h.order():
+    def sectors_out(self, slabs, i):
+        h = self.here
+        for dy, dx in slabs:
             r = h.at(dy, dx)
 
             @pl.when(h.s + 1 < h.sectors)
@@ -185,7 +189,7 @@
 
         @pl.loop(0, SLICES)
         def _(i):
-            for dy, dx in h.order():
+            for dy, dx in h.corners + h.sides:
                 r = h.at(dy, dx)
 
                 @pl.when(h.s + 1 < h.sectors)
@@ -282,7 +286,7 @@
 EXCHANGE_REFS, GATHER_REFS = 20, 8
 
 
-def kernel(target, count, wave_hbm, precond_hbm, left_hbm, right_hbm, first_out, correction_out, second_out, *scratch):
+def kernel(target_hbm, count_hbm, wave_hbm, precond_hbm, left_hbm, right_hbm, first_out, correction_out, second_out, *scratch):
     scratch = list(scratch)
 
     def take(n):
@@ -292,172 +296,238 @@
 
     here = Place()
     first, second = Exchange(here, take(EXCHANGE_REFS)), Exchange(here, take(EXCHANGE_REFS))
-    wave, precond, image, left, right, r_high, r_low, v_high, v_low = take(9)
+    wave, precond, image, left, right, r_high, r_low, v_high, v_low, in_high, in_low, target, count = take(13)
     p_gather, f_gather = Gather(here, precond, take(GATHER_REFS), 1), Gather(here, image, take(GATHER_REFS), SLICES)
-    mine, mid, term_in, sector_in, ts_s, ts_r, ss_s, ss_r, load = take(9)
+    sums, mine, theirs, all_s, all_r, load = take(6)
     terms, sectors, t, s = here.terms, here.sectors, here.t, here.s
     slots, _, rows, width = left.shape
     sub = rows // SLICES
-
-    loads = [pltpu.make_async_copy(precond_hbm, precond.at[t], load.at[0]),
-             pltpu.make_async_copy(wave_hbm, wave, load.at[1])]
-    for j in range(slots):
-        loads.append(pltpu.make_async_copy(right_hbm.at[j], right.at[j], load.at[2 + 2 * j]))
-        loads.append(pltpu.make_async_copy(left_hbm.at[j], left.at[j], load.at[3 + 2 * j]))
+    peers = terms * sectors - 1
+
+    order = here.corners + here.sides
+    load_precond = pltpu.make_async_copy(precond_hbm, precond.at[t], load.at[0])
+    load_wave = pltpu.make_async_copy(wave_hbm, wave, load.at[1])
+    load_target = pltpu.make_async_copy(target_hbm, target, load.at[2])
+    load_count = pltpu.make_async_copy(count_hbm, count, load.at[3])
+    load_right = [pltpu.make_async_copy(right_hbm.at[j], right.at[j], load.at[4 + j]) for j in range(slots)]
+    load_left = [pltpu.make_async_copy(left_hbm.at[:, here.at(*o)], left.at[:, here.at(*o)], load.at[4 + slots + n])
+                 for n, o in enumerate(order)]
+    corners = len(here.corners)
     arrived = barrier(here)
-    for copy in loads:
+    for copy in [load_precond, load_wave, load_target, load_count] + load_left[:corners] + load_right + load_left[corners:]:
         copy.start()
-    loads[0].wait()
-    arrived()
-    p_gather.begin(0)
-    loads[1].wait()
-    for r in range(terms):
-        v_high[r * rows : (r + 1) * rows], v_low[r * rows : (r + 1) * rows] = split(wave[r])
-    for j in range(slots):
-        loads[2 + 2 * j].wait()
-        r_high[j], r_low[j] = split(right[j])
-    for j in range(slots):
-        loads[3 + 2 * j].wait()
-
-    def compute(exchange, i):
-        part = pl.ds(pl.multiple_of(i * sub, sub), sub)
+
+    def split_rows(value):
+        for r in range(terms):
+            v_high[r * rows : (r + 1) * rows], v_low[r * rows : (r + 1) * rows] = split(value(r))
+
+    def inner(slabs, part):
+        stack = jnp.concatenate([left[j, here.at(*o), part] for j in range(slots) for o in slabs], axis=0)
+        return split(product(*split(stack), v_high[...], v_low[...]))
+
+    def chosen(j, p, tile):
+        hit = jnp.logical_and(j < count[0, 0], target[0, j] - s + 1 == p)
+        return jnp.where(hit, tile, 0.0)
+
+    def compute(exchange, slabs, part, size):
+        high, low = inner(slabs, part)
+        m = len(slabs) * size
+        tiles = [product(high[j * m : (j + 1) * m], low[j * m : (j + 1) * m], r_high[j], r_low[j]) for j in range(slots)]
+        for n, o in enumerate(slabs):
+            for p in range(3):
+                exchange.whole[p, here.at(*o), part] = sum(
+                    chosen(j, p, tiles[j][n * size : (n + 1) * size]) for j in range(slots))
+
+    every = pl.ds(0, rows)
+
+    def corners_first(exchange):
+        m = corners * rows
+        with jax.named_scope("startv"):
+            load_wave.wait()
+            split_rows(lambda r: wave[r])
+        with jax.named_scope("startl"):
+            for copy in load_left[:corners]:
+                copy.wait()
+            in_high[...], in_low[...] = inner(here.corners, every)
+        load_target.wait()
+        load_count.wait()
         for j in range(slots):
-            place = target[0, j] - s + 1
-            alive = j < count[0, 0]
-            left_high, left_low = split(left[j, :, part, :].reshape(terms * sub, width))
-            inner = product(left_high, left_low, v_high[...], v_low[...])
-            in_high, in_low = split(inner)
-            tile = product(in_high, in_low, r_high[j], r_low[j]).reshape(terms, sub, width)
-            for p in range(3):
-                chosen = jnp.where(jnp.logical_and(alive, place == p), tile, 0.0)
-                if j == 0:
-                    exchange.whole[p, :, part, :] = chosen
-                else:
-                    exchange.whole[p, :, part, :] += chosen
-
-    def apply(exchange, finished, relayed):
-        @pl.loop(0, SLICES + 3)
+            with jax.named_scope("startr"):
+                load_right[j].wait()
+                r_high[j], r_low[j] = split(right[j])
+            tile = product(in_high[j * m : (j + 1) * m], in_low[j * m : (j + 1) * m], r_high[j], r_low[j])
+            for n, o in enumerate(here.corners):
+                for p in range(3):
+                    part = chosen(j, p, tile[n * rows : (n + 1) * rows])
+                    exchange.whole[p, here.at(*o)] = part if j == 0 else exchange.whole[p, here.at(*o)] + part
+
+    def apply(exchange, begin, finished, relayed):
+        with jax.named_scope("CD"):
+            begin()
+        for i in range(SLICES):
+            exchange.sectors_out(here.corners, i)
+
+        @pl.loop(0, SLICES + 4)
         def _(i):
             @pl.when(i < SLICES)
             def _():
-                compute(exchange, i)
-                exchange.sectors_out(i)
-
-            @pl.when(jnp.logical_and(i >= 1, i < SLICES + 1))
+                with jax.named_scope("C"):
+                    compute(exchange, here.sides, exchange.part(i), sub)
+                with jax.named_scope("S"):
+                    exchange.sectors_out(here.sides, i)
+
+            @pl.when(jnp.logical_and(i >= 1, i < 1 + SLICES // 2))
             def _():
-                exchange.corners(i - 1)
+                with jax.named_scope("Fd"):
+                    exchange.corners(2 * i - 2)
+                    exchange.corners(2 * i - 1)
+
+            @pl.when(i >= 4)
+            def _():
+                with jax.named_scope("Fo"):
+                    finished(i - 4, exchange.own(i - 4))
 
             @pl.when(jnp.logical_and(i >= 2, i < SLICES + 2))
             def _():
-                exchange.sides(i - 2)
-
-            @pl.when(i >= 3)
-            def _():
-                finished(i - 3, exchange.own(i - 3))
+                with jax.named_scope("Fxy"):
+                    exchange.sides(i - 2)
 
             relayed(i)
 
-    def first_done(i, total):
+    def fold(x):
+        x = jnp.sum(x.reshape(sub // 8, 8, width), axis=0)
+        return sum(x[:, c : c + 128] for c in range(0, width, 128))
+
+    def first_begin():
+        corners_first(first)
+        for copy in load_left[corners:]:
+            copy.wait()
+
+    def first_done(i, f):
         part = first.part(i)
-        image[t, part] = total
-        first_out[part] = total
+        image[t, part] = f
         f_gather.begin(i)
+        first_out[part] = f
+        w, p = wave[t, part], precond[t, part]
+        wf, ww = w * f, w * w
+        for n, x in enumerate((wf, ww, wf * p, ww * p)):
+            sums[n] += fold(x)
 
     def relays(i):
-        @pl.when(i == 2)
+        @pl.when(i == 3)
         def _():
-            p_gather.relay(0)
-
-        @pl.when(i >= 5)
+            with jax.named_scope("Gp"):
+                p_gather.relay(0)
+
+        @pl.when(i >= 6)
         def _():
-            f_gather.relay(i - 5)
-
-    apply(first, first_done, relays)
-
-    w, f, p = wave[t], image[t], precond[t]
-    wf, ww = w * f, w * w
-
-    def lanes(x):
-        line = jnp.sum(x, axis=0, keepdims=True)
-        return sum(line[:, c : c + 128] for c in range(0, line.shape[1], 128))
-
-    mine[...] = jnp.zeros_like(mine)
-    for i, x in enumerate((wf, ww, wf * p, ww * p)):
-        mine[i : i + 1] = lanes(x)
-
-    def to_term(k):
-        return send(mine, term_in.at[k - 1], ts_s.at[k - 1], ts_r.at[k - 1], term=lax.rem(t + k, terms))
-
-    def to_sector(k):
-        return send(mid, sector_in.at[k - 1], ss_s.at[k - 1], ss_r.at[k - 1], sector=lax.rem(s + k, sectors))
-
-    for k in range(1, terms):
-        to_term(k).start()
-    f_gather.relay(2)
-    total = mine[...]
-    for k in range(1, terms):
-        to_term(k).wait_recv()
-        total += term_in[k - 1]
-    mid[...] = total
-    for k in range(1, sectors):
-        to_sector(k).start()
-    f_gather.relay(3)
-    p_gather.finish(0)
-    for k in range(1, sectors):
-        to_sector(k).wait_recv()
-        total += sector_in[k - 1]
-    cross, norm, a, b = (jnp.sum(total[i : i + 1], axis=1, keepdims=True) for i in range(4))
+            with jax.named_scope("Gf"):
+                f_gather.relay(i - 6)
+
+    with jax.named_scope("enter"):
+        load_precond.wait()
+        arrived()
+        p_gather.begin(0)
+    sums[...] = jnp.zeros_like(sums)
+    apply(first, first_begin, first_done, relays)
+
+    def to_peer(k):
+        return send(mine, theirs.at[k - 1], all_s.at[k - 1], all_r.at[k - 1], **here.peer(k))
+
+    lane = lax.broadcasted_iota(jnp.int32, (1, 128), 1)
+    row = jnp.zeros((1, 128), F32)
+    for n in range(4):
+        row = jnp.where(lane == n, jnp.sum(sums[n], keepdims=True), row)
+    mine[...] = row
+
+    @pl.loop(1, peers + 1)
+    def _(k):
+        to_peer(k).start()
+
+    with jax.named_scope("relay2"):
+        f_gather.relay(2)
+        f_gather.relay(3)
+        p_gather.finish(0)
+    with jax.named_scope("peers"):
+        @pl.loop(1, peers + 1)
+        def _(k):
+            to_peer(k).wait_recv()
+
+    total = mine[...] + jnp.sum(theirs[...], axis=0)
+    cross, norm, a, b = (total[:, n : n + 1] for n in range(4))
     rayleigh = cross / norm
     share = (a - rayleigh * b) / norm
-    for i in range(SLICES):
-        f_gather.finish(i)
+    with jax.named_scope("gfin"):
+        for i in range(SLICES):
+            f_gather.finish(i)
 
     def corrected(r):
         return precond[r] * (image[r] - rayleigh * wave[r]) - share * wave[r]
 
-    for r in range(terms):
-        v_high[r * rows : (r + 1) * rows], v_low[r * rows : (r + 1) * rows] = split(corrected(r))
-    correction_out[...] = corrected(t)
+    with jax.named_scope("corr"):
+        split_rows(corrected)
+        correction_out[...] = corrected(t)
 
     def second_done(i, total):
         second_out[second.part(i)] = total
 
-    apply(second, second_done, lambda i: None)
-
-    first.drain()
-    second.drain()
-    p_gather.drain()
-    f_gather.drain()
-    for k in range(1, terms):
-        to_term(k).wait_send()
-    for k in range(1, sectors):
-        to_sector(k).wait_send()
+    apply(second, lambda: compute(second, here.corners, every, rows), second_done, lambda i: None)
+
+    with jax.named_scope("drain"):
+        first.drain()
+        second.drain()
+        p_gather.drain()
+        f_gather.drain()
+
+        @pl.loop(1, peers + 1)
+        def _(k):
+            to_peer(k).wait_send()
+
+
+def publish_kernel(*refs):
+    ins, outs, sems = refs[:3], refs[3:6], refs[6]
+    copies = [pltpu.make_async_copy(a, b, sems.at[n]) for n, (a, b) in enumerate(zip(ins, outs))]
+    for copy in copies:
+        copy.start()
+    for copy in copies:
+        copy.wait()
 
 
 def per_device(wavefunction, precond, left_ops, right_ops, out_sector, live_counts):
     terms, sectors = lax.axis_size("term"), lax.axis_size("sector")
     width, slots = wavefunction.shape[1], left_ops.shape[1]
     rows = width // terms
+    gy, gx = grid_of(terms)
     dma = pltpu.SemaphoreType.DMA
     slab = jax.ShapeDtypeStruct((rows, width), F32)
     block = pltpu.VMEM((terms, rows, width), F32)
     half = pltpu.VMEM((width, width), BF16)
     operators = pltpu.VMEM((slots, terms, rows, width), F32)
     halves = pltpu.VMEM((slots, width, width), BF16)
-    tile = pltpu.VMEM((8, 128), F32)
+    inner = pltpu.VMEM((slots * (gy - 1) * (gx - 1) * rows, width), BF16)
+    peers = terms * sectors - 1
     outs = pl.pallas_call(
         kernel,
-        out_shape=(slab,) * 3,
-        in_specs=[SMEM] * 2 + [ANY] * 4,
+        out_shape=(pltpu.VMEM((rows, width), F32),) * 3,
+        in_specs=[HBM] * 6,
         out_specs=(VMEM,) * 3,
         scratch_shapes=Exchange.scratch(width, terms) * 2
-        + [block, block, block, operators, pltpu.VMEM((slots, width, width), F32), halves, halves, half, half]
+        + [block, block, block, operators, pltpu.VMEM((slots, width, width), F32), halves, halves, half, half, inner, inner,
+           pltpu.SMEM(out_sector.shape, jnp.int32), pltpu.SMEM(live_counts.shape, jnp.int32)]
         + Gather.scratch(terms, 1) + Gather.scratch(terms, SLICES)
-        + [tile, tile, pltpu.VMEM((terms - 1, 8, 128), F32), pltpu.VMEM((sectors - 1, 8, 128), F32),
-           dma((terms - 1,)), dma((terms - 1,)), dma((sectors - 1,)), dma((sectors - 1,)), dma((2 + 2 * slots,))],
-        compiler_params=pltpu.CompilerParams(collective_id=0, has_side_effects=True, vmem_limit_bytes=60 << 20),
+        + [pltpu.VMEM((4, 8, 128), F32), pltpu.VMEM((1, 128), F32), pltpu.VMEM((peers, 1, 128), F32),
+           dma((peers,)), dma((peers,)), dma((4 + slots + terms,))],
+        compiler_params=pltpu.CompilerParams(collective_id=0, has_side_effects=True, vmem_limit_bytes=VMEM_BYTES - 3 * 4 * rows * width - (192 << 10)),
     )(out_sector, live_counts, wavefunction.reshape(terms, rows, width), precond[0],
       left_ops.reshape(slots, terms, rows, width), right_ops[0])
+    outs = pl.pallas_call(
+        publish_kernel,
+        out_shape=(slab,) * 3,
+        in_specs=[VMEM] * 3,
+        out_specs=(HBM,) * 3,
+        scratch_shapes=[dma((3,))],
+        compiler_params=pltpu.CompilerParams(vmem_limit_bytes=1 << 20),
+    )(*outs)
     return tuple(x[None] for x in outs)
 
 

time: 71.9 us -> 63.7 us (0.89)
  local copies, waits for them, and re-layouts: 5.01 us -> 0 us
  Pallas kernels: 65.4 us -> 62.2 us
    unnamed x3 -> x0, local copies, waits for them, and re-layouts: 5.01 us -> none
    pallas_call x1 -> x2, Pallas kernels: 65.4 us -> 62.2 us  [the longest x1 61.3 us: per_device(): pl.pallas_call(kernel, out_shape=(pltpu.VMEM((rows, width), F32),) * 3, i...]
where the time goes in v2:
time: 63.7 us; the launch traced here: 63.5 us
  Pallas kernels  62.2 us (98%)
  between operations  1.29 us (2%)
    pallas_call x1, Pallas kernels, per_device(): pl.pallas_call(kernel, out_shape=(pltpu.VMEM((rows, width), F32),) * 3, i...  61.3 us

profile of v2, /device:TPU:0, one launch (start us, length us, event | category | flops | bytes accessed | tf_op | source)
XLA Modules:
  0.0 63.5 jit_solution(3360551320066195393)
XLA Ops:
  1.3 61.3 %shard_map.85 = (f32[128,512]{1,0:T(8,128)S(1)}, f32[128,512]{1,0:T(8,128)S(1)}, f32[128,512]{1,0:T(8,128)S(1)}) custom-call(s32[1,4]{1,0:T(1,128)} %target_hbm.1, s32[1,1]{1,0:T(1,128)S(6)} %copy.9.count_hbm, f32[4,128,512]{2,1,0:T(8,128)} %bitcast.9, f32[128,512]{1,0:T(8,128)} %bitcast.10, f32[4,4,128,512]{3,2,1,0:T(8,128)} %bitcast.7, f32[4,512,512]{2,1,0:T(8,128)} %bitcast.8), custom_call_target="tpu_custom_call" | custom-call | tf_op jit(solution)/shard_map/pallas_call | solution.py:509
  62.6 0.9 %shard_map.86 = (f32[128,512]{1,0:T(8,128)}, f32[128,512]{1,0:T(8,128)}, f32[128,512]{1,0:T(8,128)}) custom-call(f32[128,512]{1,0:T(8,128)S(1)} %get-tuple-element.9.refs_0_, f32[128,512]{1,0:T(8,128)S(1)} %get-tuple-element.10.refs_1_, f32[128,512]{1,0:T(8,128)S(1)} %get-tuple-element.11.refs_2_), custom_call_target="tpu_custom_call" | custom-call | tf_op jit(solution)/shard_map/pallas_call | solution.py:523

commit v3 on v2

--- a/solution.py
+++ b/solution.py
@@ -50,6 +50,9 @@
     def at(self, dy, dx):
         return lax.rem(self.y + dy, self.gy) * self.gx + lax.rem(self.x + dx, self.gx)
 
+    def corner(self, dy, dx):
+        return (dy - 1) * (self.gx - 1) + dx - 1
+
     def peer(self, k):
         return {"term": lax.rem(self.t + k // self.sectors, self.terms),
                 "sector": lax.rem(self.s + lax.rem(k, self.sectors), self.sectors)}
@@ -67,57 +70,61 @@
 
 
 class Exchange:
-    def __init__(self, here, refs):
+    def __init__(self, here, refs, sems):
         self.here = here
-        (self.whole, self.up_in, self.down_in, self.acc, self.da_in, self.db_in, self.x_in, self.y_in,
-         self.up_s, self.up_r, self.down_s, self.down_r, self.da_s, self.da_r, self.db_s, self.db_r,
-         self.x_s, self.x_r, self.y_s, self.y_r) = refs
+        self.whole, self.up_in, self.down_in, self.acc, self.da_in, self.db_in, self.x_in, self.y_in = refs
+        (self.z_s, self.up_r, self.down_r, self.da_s, self.da_r, self.db_s, self.db_r,
+         self.x_s, self.x_r, self.y_s, self.y_r) = sems
         self.rows, self.width = self.acc.shape[1], self.acc.shape[2]
         self.sub, self.half = self.rows // SLICES, self.width // 2
 
     @staticmethod
-    def scratch(width, terms):
+    def buffers(width, terms):
         rows, half = width // terms, width // 2
         gy, gx = grid_of(terms)
-        dma = pltpu.SemaphoreType.DMA
         whole = pltpu.VMEM((terms, rows, width), F32)
-        return [
-            pltpu.VMEM((3, terms, rows, width), F32), whole, whole, whole,
-            pltpu.VMEM((gy, gx, rows, half), F32), pltpu.VMEM((gy, gx, rows, half), F32),
-            pltpu.VMEM((gx, rows, width), F32), pltpu.VMEM((gy, rows, width), F32),
-        ] + [dma((SLICES, terms))] * 4 + [dma((SLICES, gy, gx))] * 4 + [dma((SLICES, gx))] * 2 + [dma((SLICES, gy))] * 2
+        corner = pltpu.VMEM(((gy - 1) * (gx - 1), rows, half), F32)
+        return [pltpu.VMEM((3, terms, rows, width), F32), whole, whole, whole, corner, corner,
+                pltpu.VMEM((gx - 1, rows, width), F32), pltpu.VMEM((gy - 1, rows, width), F32)]
+
+    @staticmethod
+    def semaphores(terms):
+        gy, gx = grid_of(terms)
+        dma, corners = pltpu.SemaphoreType.DMA, (gy - 1) * (gx - 1)
+        return [dma((2,)), dma((SLICES, terms)), dma((SLICES, terms))] + [dma((corners,)), dma((SLICES, corners))] * 2 + [
+            dma((gx - 1,)), dma((SLICES, gx - 1)), dma((gy - 1,)), dma((SLICES, gy - 1))]
 
     def part(self, i):
         return pl.ds(pl.multiple_of(i * self.sub, self.sub), self.sub)
 
     def upward(self, r, i):
         h = self.here
-        return send(self.whole.at[2, r, self.part(i)], self.up_in.at[r, self.part(i)], self.up_s.at[i, r],
+        return send(self.whole.at[2, r, self.part(i)], self.up_in.at[r, self.part(i)], self.z_s.at[1],
                     self.up_r.at[i, r], sector=lax.rem(h.s + 1, h.sectors))
 
     def downward(self, r, i):
         h = self.here
-        return send(self.whole.at[0, r, self.part(i)], self.down_in.at[r, self.part(i)], self.down_s.at[i, r],
+        return send(self.whole.at[0, r, self.part(i)], self.down_in.at[r, self.part(i)], self.z_s.at[0],
                     self.down_r.at[i, r], sector=lax.rem(h.s + h.sectors - 1, h.sectors))
 
     def corner_a(self, dy, dx, i):
-        h, part = self.here, self.part(i)
-        return send(self.acc.at[h.at(dy, dx), part, : self.half], self.da_in.at[dy, dx, part],
-                    self.da_s.at[i, dy, dx], self.da_r.at[i, dy, dx], term=h.at(0, dx))
+        h, part, c = self.here, self.part(i), self.here.corner(dy, dx)
+        return send(self.acc.at[h.at(dy, dx), part, : self.half], self.da_in.at[c, part],
+                    self.da_s.at[c], self.da_r.at[i, c], term=h.at(0, dx))
 
     def corner_b(self, dy, dx, i):
-        h, part = self.here, self.part(i)
-        return send(self.acc.at[h.at(dy, dx), part, self.half :], self.db_in.at[dy, dx, part],
-                    self.db_s.at[i, dy, dx], self.db_r.at[i, dy, dx], term=h.at(dy, 0))
+        h, part, c = self.here, self.part(i), self.here.corner(dy, dx)
+        return send(self.acc.at[h.at(dy, dx), part, self.half :], self.db_in.at[c, part],
+                    self.db_s.at[c], self.db_r.at[i, c], term=h.at(dy, 0))
 
     def along_x(self, dx, i):
         h, part = self.here, self.part(i)
-        return send(self.acc.at[h.at(0, dx), part], self.x_in.at[dx, part], self.x_s.at[i, dx], self.x_r.at[i, dx],
+        return send(self.acc.at[h.at(0, dx), part], self.x_in.at[dx - 1, part], self.x_s.at[dx - 1], self.x_r.at[i, dx - 1],
                     term=h.at(0, dx))
 
     def along_y(self, dy, i):
         h, part = self.here, self.part(i)
-        return send(self.acc.at[h.at(dy, 0), part], self.y_in.at[dy, part], self.y_s.at[i, dy], self.y_r.at[i, dy],
+        return send(self.acc.at[h.at(dy, 0), part], self.y_in.at[dy - 1, part], self.y_s.at[dy - 1], self.y_r.at[i, dy - 1],
                     term=h.at(dy, 0))
 
     def sectors_out(self, slabs, i):
@@ -162,14 +169,14 @@
             self.merge(r, i)
             for dx in range(1, h.gx):
                 self.corner_a(dy, dx, i).wait_recv()
-                self.acc[r, part, : self.half] += self.da_in[dy, dx, part]
+                self.acc[r, part, : self.half] += self.da_in[h.corner(dy, dx), part]
             self.along_y(dy, i).start()
         for dx in range(1, h.gx):
             r = h.at(0, dx)
             self.merge(r, i)
             for dy in range(1, h.gy):
                 self.corner_b(dy, dx, i).wait_recv()
-                self.acc[r, part, self.half :] += self.db_in[dy, dx, part]
+                self.acc[r, part, self.half :] += self.db_in[h.corner(dy, dx), part]
             self.along_x(dx, i).start()
 
     def own(self, i):
@@ -178,35 +185,34 @@
         total = self.acc[h.t, part]
         for dy in range(1, h.gy):
             self.along_y(dy, i).wait_recv()
-            total += self.y_in[dy, part]
+            total += self.y_in[dy - 1, part]
         for dx in range(1, h.gx):
             self.along_x(dx, i).wait_recv()
-            total += self.x_in[dx, part]
+            total += self.x_in[dx - 1, part]
         return total
 
     def drain(self):
         h = self.here
 
-        @pl.loop(0, SLICES)
-        def _(i):
-            for dy, dx in h.corners + h.sides:
-                r = h.at(dy, dx)
-
-                @pl.when(h.s + 1 < h.sectors)
-                def _():
-                    self.upward(r, i).wait_send()
-
-                @pl.when(h.s > 0)
-                def _():
-                    self.downward(r, i).wait_send()
-
-                if dy and dx:
-                    self.corner_a(dy, dx, i).wait_send()
-                    self.corner_b(dy, dx, i).wait_send()
-                elif dy:
-                    self.along_y(dy, i).wait_send()
-                elif dx:
-                    self.along_x(dx, i).wait_send()
+        def sent(source, target, sem):
+            send(source, target, sem, self.up_r.at[0, 0], term=h.at(0, 1), sector=h.s).wait_send()
+
+        @pl.when(h.s + 1 < h.sectors)
+        def _():
+            sent(self.whole.at[2], self.up_in, self.z_s.at[1])
+
+        @pl.when(h.s > 0)
+        def _():
+            sent(self.whole.at[0], self.down_in, self.z_s.at[0])
+
+        for dy, dx in h.corners:
+            c = h.corner(dy, dx)
+            sent(self.da_in.at[c], self.da_in.at[c], self.da_s.at[c])
+            sent(self.db_in.at[c], self.db_in.at[c], self.db_s.at[c])
+        for n in range(h.gx - 1):
+            sent(self.x_in.at[n], self.x_in.at[n], self.x_s.at[n])
+        for n in range(h.gy - 1):
+            sent(self.y_in.at[n], self.y_in.at[n], self.y_s.at[n])
 
 
 class Gather:
@@ -220,26 +226,28 @@
     def scratch(terms, pieces):
         gy, gx = grid_of(terms)
         dma = pltpu.SemaphoreType.DMA
-        return [dma((pieces, gx))] * 2 + [dma((pieces, gy))] * 2 + [dma((pieces, gy, gx))] * 4
+        corners = (gy - 1) * (gx - 1)
+        return [dma((gx - 1,)), dma((pieces, gx - 1)), dma((gy - 1,)), dma((pieces, gy - 1))] + [
+            dma((corners,)), dma((pieces, corners))] * 2
 
     def part(self, i):
         return pl.ds(pl.multiple_of(i * self.sub, self.sub), self.sub)
 
     def to_x(self, r, dx, i):
         ref = self.full.at[r, self.part(i)]
-        return send(ref, ref, self.x_s.at[i, dx], self.x_r.at[i, dx], term=self.here.at(0, dx))
+        return send(ref, ref, self.x_s.at[dx - 1], self.x_r.at[i, dx - 1], term=self.here.at(0, dx))
 
     def to_y(self, r, dy, i):
         ref = self.full.at[r, self.part(i)]
-        return send(ref, ref, self.y_s.at[i, dy], self.y_r.at[i, dy], term=self.here.at(dy, 0))
+        return send(ref, ref, self.y_s.at[dy - 1], self.y_r.at[i, dy - 1], term=self.here.at(dy, 0))
 
     def relay_a(self, r, dy, dx, i):
-        ref = self.full.at[r, self.part(i), : self.half]
-        return send(ref, ref, self.a_s.at[i, dy, dx], self.a_r.at[i, dy, dx], term=self.here.at(0, dx))
+        ref, c = self.full.at[r, self.part(i), : self.half], self.here.corner(dy, dx)
+        return send(ref, ref, self.a_s.at[c], self.a_r.at[i, c], term=self.here.at(0, dx))
 
     def relay_b(self, r, dy, dx, i):
-        ref = self.full.at[r, self.part(i), self.half :]
-        return send(ref, ref, self.b_s.at[i, dy, dx], self.b_r.at[i, dy, dx], term=self.here.at(dy, 0))
+        ref, c = self.full.at[r, self.part(i), self.half :], self.here.corner(dy, dx)
+        return send(ref, ref, self.b_s.at[c], self.b_r.at[i, c], term=self.here.at(dy, 0))
 
     def begin(self, i):
         h = self.here
@@ -271,19 +279,19 @@
     def drain(self):
         h = self.here
 
-        @pl.loop(0, self.pieces)
-        def _(i):
-            for dx in range(1, h.gx):
-                self.to_x(h.t, dx, i).wait_send()
-            for dy in range(1, h.gy):
-                self.to_y(h.t, dy, i).wait_send()
-            for dy in range(1, h.gy):
-                for dx in range(1, h.gx):
-                    self.relay_a(h.at(dy, 0), dy, dx, i).wait_send()
-                    self.relay_b(h.at(0, dx), dy, dx, i).wait_send()
-
-
-EXCHANGE_REFS, GATHER_REFS = 20, 8
+        def sent(ref, sem):
+            send(ref, ref, sem, self.x_r.at[0, 0], term=h.at(0, 1)).wait_send()
+
+        for n in range(h.gx - 1):
+            sent(self.full.at[h.t], self.x_s.at[n])
+        for n in range(h.gy - 1):
+            sent(self.full.at[h.t], self.y_s.at[n])
+        for dy, dx in h.corners:
+            sent(self.full.at[h.at(dy, 0), :, : self.half], self.a_s.at[h.corner(dy, dx)])
+            sent(self.full.at[h.at(0, dx), :, self.half :], self.b_s.at[h.corner(dy, dx)])
+
+
+BUFFERS, SEMAPHORES, GATHER_REFS = 8, 11, 8
 
 
 def kernel(target_hbm, count_hbm, wave_hbm, precond_hbm, left_hbm, right_hbm, first_out, correction_out, second_out, *scratch):
@@ -295,7 +303,8 @@
         return refs
 
     here = Place()
-    first, second = Exchange(here, take(EXCHANGE_REFS)), Exchange(here, take(EXCHANGE_REFS))
+    buffers, more, sems = take(BUFFERS), take(BUFFERS), take(SEMAPHORES)
+    first, second = Exchange(here, buffers, sems), Exchange(here, more, sems)
     wave, precond, image, left, right, r_high, r_low, v_high, v_low, in_high, in_low, target, count = take(13)
     p_gather, f_gather = Gather(here, precond, take(GATHER_REFS), 1), Gather(here, image, take(GATHER_REFS), SLICES)
     sums, mine, theirs, all_s, all_r, load = take(6)
@@ -351,15 +360,21 @@
             in_high[...], in_low[...] = inner(here.corners, every)
         load_target.wait()
         load_count.wait()
-        for j in range(slots):
+        pairs = [range(j, min(j + 2, slots)) for j in range(0, slots, 2)]
+        for pair in pairs:
             with jax.named_scope("startr"):
-                load_right[j].wait()
-                r_high[j], r_low[j] = split(right[j])
-            tile = product(in_high[j * m : (j + 1) * m], in_low[j * m : (j + 1) * m], r_high[j], r_low[j])
-            for n, o in enumerate(here.corners):
-                for p in range(3):
-                    part = chosen(j, p, tile[n * rows : (n + 1) * rows])
-                    exchange.whole[p, here.at(*o)] = part if j == 0 else exchange.whole[p, here.at(*o)] + part
+                for j in pair:
+                    load_right[j].wait()
+                tiles = {}
+                for j in pair:
+                    high, low = split(right[j])
+                    r_high[j], r_low[j] = high, low
+                    tiles[j] = product(in_high[j * m : (j + 1) * m], in_low[j * m : (j + 1) * m], high, low)
+                for n, o in enumerate(here.corners):
+                    for p in range(3):
+                        part = sum(chosen(j, p, tiles[j][n * rows : (n + 1) * rows]) for j in pair)
+                        ref = exchange.whole.at[p, here.at(*o)]
+                        ref[...] = part if pair == pairs[0] else ref[...] + part
 
     def apply(exchange, begin, finished, relayed):
         with jax.named_scope("CD"):
@@ -382,18 +397,18 @@
                     exchange.corners(2 * i - 2)
                     exchange.corners(2 * i - 1)
 
+            relayed(i)
+
+            @pl.when(jnp.logical_and(i >= 2, i < SLICES + 2))
+            def _():
+                with jax.named_scope("Fxy"):
+                    exchange.sides(i - 2)
+
             @pl.when(i >= 4)
             def _():
                 with jax.named_scope("Fo"):
                     finished(i - 4, exchange.own(i - 4))
 
-            @pl.when(jnp.logical_and(i >= 2, i < SLICES + 2))
-            def _():
-                with jax.named_scope("Fxy"):
-                    exchange.sides(i - 2)
-
-            relayed(i)
-
     def fold(x):
         x = jnp.sum(x.reshape(sub // 8, 8, width), axis=0)
         return sum(x[:, c : c + 128] for c in range(0, width, 128))
@@ -406,7 +421,15 @@
     def first_done(i, f):
         part = first.part(i)
         image[t, part] = f
-        f_gather.begin(i)
+
+        @pl.when(i == 1)
+        def _():
+            f_gather.begin(0)
+
+        @pl.when(i >= 1)
+        def _():
+            f_gather.begin(i)
+
         first_out[part] = f
         w, p = wave[t, part], precond[t, part]
         wf, ww = w * f, w * w
@@ -414,15 +437,10 @@
             sums[n] += fold(x)
 
     def relays(i):
-        @pl.when(i == 3)
+        @pl.when(i == 2)
         def _():
             with jax.named_scope("Gp"):
                 p_gather.relay(0)
-
-        @pl.when(i >= 6)
-        def _():
-            with jax.named_scope("Gf"):
-                f_gather.relay(i - 6)
 
     with jax.named_scope("enter"):
         load_precond.wait()
@@ -432,26 +450,25 @@
     apply(first, first_begin, first_done, relays)
 
     def to_peer(k):
-        return send(mine, theirs.at[k - 1], all_s.at[k - 1], all_r.at[k - 1], **here.peer(k))
-
-    lane = lax.broadcasted_iota(jnp.int32, (1, 128), 1)
-    row = jnp.zeros((1, 128), F32)
-    for n in range(4):
-        row = jnp.where(lane == n, jnp.sum(sums[n], keepdims=True), row)
-    mine[...] = row
-
-    @pl.loop(1, peers + 1)
-    def _(k):
-        to_peer(k).start()
+        return send(mine, theirs.at[k - 1], all_s.at[0], all_r.at[0], **here.peer(k))
+
+    all_peers = send(theirs, theirs, all_s.at[0], all_r.at[0], **here.peer(1))
+    with jax.named_scope("sums"):
+        shape = (4, 128)
+        diagonal = lax.broadcasted_iota(jnp.int32, shape, 0) == lax.broadcasted_iota(jnp.int32, shape, 1)
+        line = jnp.sum(jnp.sum(sums[...], axis=1), axis=1, keepdims=True)
+        mine[...] = jnp.sum(jnp.where(diagonal, line, 0.0), axis=0, keepdims=True)
+
+        @pl.loop(1, peers + 1)
+        def _(k):
+            to_peer(k).start()
 
     with jax.named_scope("relay2"):
-        f_gather.relay(2)
-        f_gather.relay(3)
+        for i in range(SLICES):
+            f_gather.relay(i)
         p_gather.finish(0)
     with jax.named_scope("peers"):
-        @pl.loop(1, peers + 1)
-        def _(k):
-            to_peer(k).wait_recv()
+        all_peers.wait_recv()
 
     total = mine[...] + jnp.sum(theirs[...], axis=0)
     cross, norm, a, b = (total[:, n : n + 1] for n in range(4))
@@ -471,17 +488,14 @@
     def second_done(i, total):
         second_out[second.part(i)] = total
 
+    first.drain()
     apply(second, lambda: compute(second, here.corners, every, rows), second_done, lambda i: None)
 
     with jax.named_scope("drain"):
-        first.drain()
         second.drain()
         p_gather.drain()
         f_gather.drain()
-
-        @pl.loop(1, peers + 1)
-        def _(k):
-            to_peer(k).wait_send()
+        all_peers.wait_send()
 
 
 def publish_kernel(*refs):
@@ -511,12 +525,12 @@
         out_shape=(pltpu.VMEM((rows, width), F32),) * 3,
         in_specs=[HBM] * 6,
         out_specs=(VMEM,) * 3,
-        scratch_shapes=Exchange.scratch(width, terms) * 2
+        scratch_shapes=Exchange.buffers(width, terms) * 2 + Exchange.semaphores(terms)
         + [block, block, block, operators, pltpu.VMEM((slots, width, width), F32), halves, halves, half, half, inner, inner,
            pltpu.SMEM(out_sector.shape, jnp.int32), pltpu.SMEM(live_counts.shape, jnp.int32)]
         + Gather.scratch(terms, 1) + Gather.scratch(terms, SLICES)
         + [pltpu.VMEM((4, 8, 128), F32), pltpu.VMEM((1, 128), F32), pltpu.VMEM((peers, 1, 128), F32),
-           dma((peers,)), dma((peers,)), dma((4 + slots + terms,))],
+           dma((1,)), dma((1,)), dma((4 + slots + terms,))],
         compiler_params=pltpu.CompilerParams(collective_id=0, has_side_effects=True, vmem_limit_bytes=VMEM_BYTES - 3 * 4 * rows * width - (192 << 10)),
     )(out_sector, live_counts, wavefunction.reshape(terms, rows, width), precond[0],
       left_ops.reshape(slots, terms, rows, width), right_ops[0])

time: 63.7 us -> 57.4 us (0.901)
  Pallas kernels: 62.2 us -> 55.6 us
    pallas_call x1, Pallas kernels: 61.3 us -> 54.7 us  [per_device(): pl.pallas_call(kernel, out_shape=(pltpu.VMEM((rows, width), F32),) * 3, i...]
where the time goes in v3:
time: 57.4 us; the launch traced here: 56.9 us
  Pallas kernels  55.6 us (97%)
  between operations  1.29 us (2%)
    pallas_call x1, Pallas kernels, per_device(): pl.pallas_call(kernel, out_shape=(pltpu.VMEM((rows, width), F32),) * 3, i...  54.7 us

profile of v3, /device:TPU:0, one launch (start us, length us, event | category | flops | bytes accessed | tf_op | source)
XLA Modules:
  0.0 56.9 jit_solution(11625925330754148221)
XLA Ops:
  1.3 54.7 %shard_map.85 = (f32[128,512]{1,0:T(8,128)S(1)}, f32[128,512]{1,0:T(8,128)S(1)}, f32[128,512]{1,0:T(8,128)S(1)}) custom-call(s32[1,4]{1,0:T(1,128)} %target_hbm.1, s32[1,1]{1,0:T(1,128)S(6)} %copy.9.count_hbm, f32[4,128,512]{2,1,0:T(8,128)} %bitcast.9, f32[128,512]{1,0:T(8,128)} %bitcast.10, f32[4,4,128,512]{3,2,1,0:T(8,128)} %bitcast.7, f32[4,512,512]{2,1,0:T(8,128)} %bitcast.8), custom_call_target="tpu_custom_call" | custom-call | tf_op jit(solution)/shard_map/pallas_call | solution.py:523
  56.0 0.9 %shard_map.86 = (f32[128,512]{1,0:T(8,128)}, f32[128,512]{1,0:T(8,128)}, f32[128,512]{1,0:T(8,128)}) custom-call(f32[128,512]{1,0:T(8,128)S(1)} %get-tuple-element.9.refs_0_, f32[128,512]{1,0:T(8,128)S(1)} %get-tuple-element.10.refs_1_, f32[128,512]{1,0:T(8,128)S(1)} %get-tuple-element.11.refs_2_), custom_call_target="tpu_custom_call" | custom-call | tf_op jit(solution)/shard_map/pallas_call | solution.py:537

commit v4 on v3

--- a/solution.py
+++ b/solution.py
@@ -45,7 +45,8 @@
         self.gy, self.gx = grid_of(self.terms)
         self.y, self.x = self.t // self.gx, lax.rem(self.t, self.gx)
         self.corners = [(dy, dx) for dy in range(1, self.gy) for dx in range(1, self.gx)]
-        self.sides = [(dy, 0) for dy in range(1, self.gy)] + [(0, dx) for dx in range(1, self.gx)] + [(0, 0)]
+        self.sides = [(dy, 0) for dy in range(1, self.gy)] + [(0, dx) for dx in range(1, self.gx)]
+        self.own = [(0, 0)]
 
     def at(self, dy, dx):
         return lax.rem(self.y + dy, self.gy) * self.gx + lax.rem(self.x + dx, self.gx)
@@ -306,14 +307,14 @@
     buffers, more, sems = take(BUFFERS), take(BUFFERS), take(SEMAPHORES)
     first, second = Exchange(here, buffers, sems), Exchange(here, more, sems)
     wave, precond, image, left, right, r_high, r_low, v_high, v_low, in_high, in_low, target, count = take(13)
-    p_gather, f_gather = Gather(here, precond, take(GATHER_REFS), 1), Gather(here, image, take(GATHER_REFS), SLICES)
+    p_gather, f_gather = Gather(here, precond, take(GATHER_REFS), SLICES), Gather(here, image, take(GATHER_REFS), SLICES)
     sums, mine, theirs, all_s, all_r, load = take(6)
     terms, sectors, t, s = here.terms, here.sectors, here.t, here.s
     slots, _, rows, width = left.shape
     sub = rows // SLICES
     peers = terms * sectors - 1
 
-    order = here.corners + here.sides
+    order = here.corners + here.sides + here.own
     load_precond = pltpu.make_async_copy(precond_hbm, precond.at[t], load.at[0])
     load_wave = pltpu.make_async_copy(wave_hbm, wave, load.at[1])
     load_target = pltpu.make_async_copy(target_hbm, target, load.at[2])
@@ -326,9 +327,10 @@
     for copy in [load_precond, load_wave, load_target, load_count] + load_left[:corners] + load_right + load_left[corners:]:
         copy.start()
 
-    def split_rows(value):
+    def split_rows(value, start, size):
         for r in range(terms):
-            v_high[r * rows : (r + 1) * rows], v_low[r * rows : (r + 1) * rows] = split(value(r))
+            to = pl.ds(r * rows + start, size)
+            v_high[to], v_low[to] = split(value(r, pl.ds(start, size)))
 
     def inner(slabs, part):
         stack = jnp.concatenate([left[j, here.at(*o), part] for j in range(slots) for o in slabs], axis=0)
@@ -353,7 +355,7 @@
         m = corners * rows
         with jax.named_scope("startv"):
             load_wave.wait()
-            split_rows(lambda r: wave[r])
+            split_rows(lambda r, part: wave[r, part], 0, rows)
         with jax.named_scope("startl"):
             for copy in load_left[:corners]:
                 copy.wait()
@@ -376,38 +378,42 @@
                         ref = exchange.whole.at[p, here.at(*o)]
                         ref[...] = part if pair == pairs[0] else ref[...] + part
 
-    def apply(exchange, begin, finished, relayed):
+    def apply(exchange, begin, finished, meanwhile):
         with jax.named_scope("CD"):
             begin()
         for i in range(SLICES):
             exchange.sectors_out(here.corners, i)
-
-        @pl.loop(0, SLICES + 4)
+        meanwhile(0)
+
+        @pl.loop(0, SLICES // 2)
+        def _(b):
+            with jax.named_scope("C"):
+                compute(exchange, here.sides, pl.ds(pl.multiple_of(b * 2 * sub, 2 * sub), 2 * sub), 2 * sub)
+            exchange.sectors_out(here.sides, 2 * b)
+            exchange.sectors_out(here.sides, 2 * b + 1)
+            meanwhile(b + 1)
+
+        with jax.named_scope("Fd"):
+            for i in range(SLICES // 2):
+                exchange.corners(i)
+        with jax.named_scope("CO"):
+            compute(exchange, here.own, every, rows)
+        for i in range(SLICES):
+            exchange.sectors_out(here.own, i)
+        with jax.named_scope("Fd"):
+            for i in range(SLICES // 2, SLICES):
+                exchange.corners(i)
+        meanwhile(SLICES - 1)
+
+        @pl.loop(0, SLICES)
         def _(i):
-            @pl.when(i < SLICES)
-            def _():
-                with jax.named_scope("C"):
-                    compute(exchange, here.sides, exchange.part(i), sub)
-                with jax.named_scope("S"):
-                    exchange.sectors_out(here.sides, i)
-
-            @pl.when(jnp.logical_and(i >= 1, i < 1 + SLICES // 2))
-            def _():
-                with jax.named_scope("Fd"):
-                    exchange.corners(2 * i - 2)
-                    exchange.corners(2 * i - 1)
-
-            relayed(i)
-
-            @pl.when(jnp.logical_and(i >= 2, i < SLICES + 2))
-            def _():
-                with jax.named_scope("Fxy"):
-                    exchange.sides(i - 2)
-
-            @pl.when(i >= 4)
-            def _():
-                with jax.named_scope("Fo"):
-                    finished(i - 4, exchange.own(i - 4))
+            with jax.named_scope("Fxy"):
+                exchange.sides(i)
+
+        @pl.loop(0, SLICES)
+        def _(i):
+            with jax.named_scope("Fo"):
+                finished(i, exchange.own(i))
 
     def fold(x):
         x = jnp.sum(x.reshape(sub // 8, 8, width), axis=0)
@@ -422,11 +428,7 @@
         part = first.part(i)
         image[t, part] = f
 
-        @pl.when(i == 1)
-        def _():
-            f_gather.begin(0)
-
-        @pl.when(i >= 1)
+        @pl.when(i < SLICES - 1)
         def _():
             f_gather.begin(i)
 
@@ -436,18 +438,13 @@
         for n, x in enumerate((wf, ww, wf * p, ww * p)):
             sums[n] += fold(x)
 
-    def relays(i):
-        @pl.when(i == 2)
-        def _():
-            with jax.named_scope("Gp"):
-                p_gather.relay(0)
-
     with jax.named_scope("enter"):
         load_precond.wait()
         arrived()
-        p_gather.begin(0)
+        for i in range(SLICES):
+            p_gather.begin(i)
     sums[...] = jnp.zeros_like(sums)
-    apply(first, first_begin, first_done, relays)
+    apply(first, first_begin, first_done, p_gather.relay)
 
     def to_peer(k):
         return send(mine, theirs.at[k - 1], all_s.at[0], all_r.at[0], **here.peer(k))
@@ -464,9 +461,11 @@
             to_peer(k).start()
 
     with jax.named_scope("relay2"):
+        f_gather.begin(SLICES - 1)
+        for i in range(SLICES):
+            p_gather.finish(i)
         for i in range(SLICES):
             f_gather.relay(i)
-        p_gather.finish(0)
     with jax.named_scope("peers"):
         all_peers.wait_recv()
 
@@ -474,16 +473,16 @@
     cross, norm, a, b = (total[:, n : n + 1] for n in range(4))
     rayleigh = cross / norm
     share = (a - rayleigh * b) / norm
-    with jax.named_scope("gfin"):
-        for i in range(SLICES):
+
+    def corrected(r, part):
+        return precond[r, part] * (image[r, part] - rayleigh * wave[r, part]) - share * wave[r, part]
+
+    correction_out[...] = corrected(t, every)
+    for i in range(SLICES):
+        with jax.named_scope("gfin"):
             f_gather.finish(i)
-
-    def corrected(r):
-        return precond[r] * (image[r] - rayleigh * wave[r]) - share * wave[r]
-
-    with jax.named_scope("corr"):
-        split_rows(corrected)
-        correction_out[...] = corrected(t)
+        with jax.named_scope("corr"):
+            split_rows(corrected, i * sub, sub)
 
     def second_done(i, total):
         second_out[second.part(i)] = total
@@ -528,7 +527,7 @@
         scratch_shapes=Exchange.buffers(width, terms) * 2 + Exchange.semaphores(terms)
         + [block, block, block, operators, pltpu.VMEM((slots, width, width), F32), halves, halves, half, half, inner, inner,
            pltpu.SMEM(out_sector.shape, jnp.int32), pltpu.SMEM(live_counts.shape, jnp.int32)]
-        + Gather.scratch(terms, 1) + Gather.scratch(terms, SLICES)
+        + Gather.scratch(terms, SLICES) * 2
         + [pltpu.VMEM((4, 8, 128), F32), pltpu.VMEM((1, 128), F32), pltpu.VMEM((peers, 1, 128), F32),
            dma((1,)), dma((1,)), dma((4 + slots + terms,))],
         compiler_params=pltpu.CompilerParams(collective_id=0, has_side_effects=True, vmem_limit_bytes=VMEM_BYTES - 3 * 4 * rows * width - (192 << 10)),

time: 57.4 us -> 55.8 us (0.972)
  Pallas kernels: 55.6 us -> 54.4 us
    pallas_call x1, Pallas kernels: 54.7 us -> 53.5 us  [per_device(): pl.pallas_call(kernel, out_shape=(pltpu.VMEM((rows, width), F32),) * 3, i...]
where the time goes in v4:
time: 55.8 us; the launch traced here: 55.7 us
  Pallas kernels  54.4 us (97%)
  between operations  1.29 us (2%)
    pallas_call x1, Pallas kernels, per_device(): pl.pallas_call(kernel, out_shape=(pltpu.VMEM((rows, width), F32),) * 3, i...  53.5 us

profile of v4, /device:TPU:0, one launch (start us, length us, event | category | flops | bytes accessed | tf_op | source)
XLA Modules:
  0.0 55.7 jit_solution(3322082982634376351)
XLA Ops:
  1.3 53.5 %shard_map.85 = (f32[128,512]{1,0:T(8,128)S(1)}, f32[128,512]{1,0:T(8,128)S(1)}, f32[128,512]{1,0:T(8,128)S(1)}) custom-call(s32[1,4]{1,0:T(1,128)} %target_hbm.1, s32[1,1]{1,0:T(1,128)S(6)} %copy.9.count_hbm, f32[4,128,512]{2,1,0:T(8,128)} %bitcast.9, f32[128,512]{1,0:T(8,128)} %bitcast.10, f32[4,4,128,512]{3,2,1,0:T(8,128)} %bitcast.7, f32[4,512,512]{2,1,0:T(8,128)} %bitcast.8), custom_call_target="tpu_custom_call" | custom-call | tf_op jit(solution)/shard_map/pallas_call | solution.py:522
  54.8 0.9 %shard_map.86 = (f32[128,512]{1,0:T(8,128)}, f32[128,512]{1,0:T(8,128)}, f32[128,512]{1,0:T(8,128)}) custom-call(f32[128,512]{1,0:T(8,128)S(1)} %get-tuple-element.9.refs_0_, f32[128,512]{1,0:T(8,128)S(1)} %get-tuple-element.10.refs_1_, f32[128,512]{1,0:T(8,128)S(1)} %get-tuple-element.11.refs_2_), custom_call_target="tpu_custom_call" | custom-call | tf_op jit(solution)/shard_map/pallas_call | solution.py:536

commit v5 on v4

--- a/solution.py
+++ b/solution.py
@@ -13,6 +13,7 @@
 VMEM = pl.BlockSpec(memory_space=pltpu.VMEM)
 HBM = pl.BlockSpec(memory_space=pltpu.HBM)
 SLICES = 4
+EARLY = SLICES - 1
 VMEM_BYTES = 67043328
 
 
@@ -24,6 +25,13 @@
 def product(a_high, a_low, b_high, b_low):
     dot = functools.partial(jnp.dot, preferred_element_type=F32)
     return dot(a_high, b_high) + dot(a_high, b_low) + dot(a_low, b_high)
+
+
+def stacked(a_high, a_low, b_high, b_low):
+    dot = functools.partial(jnp.dot, preferred_element_type=F32)
+    m = a_high.shape[0]
+    both = dot(jnp.concatenate([a_high, a_low], axis=0), b_high)
+    return both[:m] + both[m:] + dot(a_high, b_low)
 
 
 def send(source, target, send_sem, recv_sem, **where):
@@ -54,25 +62,55 @@
     def corner(self, dy, dx):
         return (dy - 1) * (self.gx - 1) + dx - 1
 
-    def peer(self, k):
-        return {"term": lax.rem(self.t + k // self.sectors, self.terms),
-                "sector": lax.rem(self.s + lax.rem(k, self.sectors), self.sectors)}
+    def peers(self):
+        terms = [lax.rem(self.t + k, self.terms) for k in range(self.terms)]
+        sectors = [lax.rem(self.s + k, self.sectors) for k in range(self.sectors)]
+        pairs = [{"term": t, "sector": s} for t in terms for s in sectors]
+        return list(enumerate(pairs[1:]))
 
 
 def barrier(here):
     sem = pltpu.get_barrier_semaphore()
-    peers = here.terms * here.sectors - 1
-
-    @pl.loop(1, peers + 1)
-    def _(k):
-        pl.semaphore_signal(sem, inc=1, device_id=here.peer(k), device_id_type=MESH)
-
-    return lambda: pl.semaphore_wait(sem, peers)
+    peers = here.peers()
+    for _, where in peers:
+        pl.semaphore_signal(sem, inc=1, device_id=where, device_id_type=MESH)
+    return lambda: pl.semaphore_wait(sem, len(peers))
+
+
+class Total:
+    def __init__(self, here, refs):
+        self.here = here
+        self.sums, self.mine, self.theirs, self.send_sem, self.recv_sem = refs
+
+    @staticmethod
+    def scratch(values, peers):
+        dma = pltpu.SemaphoreType.DMA
+        return [pltpu.VMEM((values, 8, 128), F32), pltpu.VMEM((1, 128), F32), pltpu.VMEM((peers, 1, 128), F32),
+                dma((1,)), dma((1,))]
+
+    def all(self):
+        return send(self.theirs, self.theirs, self.send_sem.at[0], self.recv_sem.at[0], **self.here.peers()[0][1])
+
+    def begin(self):
+        shape = (self.sums.shape[0], 128)
+        diagonal = lax.broadcasted_iota(jnp.int32, shape, 0) == lax.broadcasted_iota(jnp.int32, shape, 1)
+        line = jnp.sum(jnp.sum(self.sums[...], axis=1), axis=1, keepdims=True)
+        self.mine[...] = jnp.sum(jnp.where(diagonal, line, 0.0), axis=0, keepdims=True)
+        for k, where in self.here.peers():
+            send(self.mine, self.theirs.at[k], self.send_sem.at[0], self.recv_sem.at[0], **where).start()
+
+    def finish(self):
+        self.all().wait_recv()
+        total = self.mine[...] + jnp.sum(self.theirs[...], axis=0)
+        return [total[:, n : n + 1] for n in range(self.sums.shape[0])]
+
+    def drain(self):
+        self.all().wait_send()
 
 
 class Exchange:
-    def __init__(self, here, refs, sems):
-        self.here = here
+    def __init__(self, here, refs, sems, tally=None):
+        self.here, self.tally = here, tally
         self.whole, self.up_in, self.down_in, self.acc, self.da_in, self.db_in, self.x_in, self.y_in = refs
         (self.z_s, self.up_r, self.down_r, self.da_s, self.da_r, self.db_s, self.db_r,
          self.x_s, self.x_r, self.y_s, self.y_r) = sems
@@ -154,6 +192,9 @@
         def _():
             self.downward(r, i).wait_recv()
             self.acc[r, part] += self.down_in[r, part]
+
+        if self.tally:
+            self.tally(r, part, self.acc[r, part])
 
     def corners(self, i):
         h = self.here
@@ -182,7 +223,6 @@
 
     def own(self, i):
         h, part = self.here, self.part(i)
-        self.merge(h.t, i)
         total = self.acc[h.t, part]
         for dy in range(1, h.gy):
             self.along_y(dy, i).wait_recv()
@@ -220,8 +260,7 @@
     def __init__(self, here, full, refs, pieces):
         self.here, self.full = here, full
         self.x_s, self.x_r, self.y_s, self.y_r, self.a_s, self.a_r, self.b_s, self.b_r = refs
-        self.sub, self.half = full.shape[1] // pieces, full.shape[2] // 2
-        self.pieces = pieces
+        self.sub, self.half, self.pieces = full.shape[1] // SLICES, full.shape[2] // 2, pieces
 
     @staticmethod
     def scratch(terms, pieces):
@@ -278,21 +317,21 @@
                 self.relay_b(h.at(h.gy - dy, dx), dy, dx, i).wait_recv()
 
     def drain(self):
-        h = self.here
+        h, all_rows = self.here, pl.ds(0, self.pieces * self.sub)
 
         def sent(ref, sem):
             send(ref, ref, sem, self.x_r.at[0, 0], term=h.at(0, 1)).wait_send()
 
         for n in range(h.gx - 1):
-            sent(self.full.at[h.t], self.x_s.at[n])
+            sent(self.full.at[h.t, all_rows], self.x_s.at[n])
         for n in range(h.gy - 1):
-            sent(self.full.at[h.t], self.y_s.at[n])
+            sent(self.full.at[h.t, all_rows], self.y_s.at[n])
         for dy, dx in h.corners:
-            sent(self.full.at[h.at(dy, 0), :, : self.half], self.a_s.at[h.corner(dy, dx)])
-            sent(self.full.at[h.at(0, dx), :, self.half :], self.b_s.at[h.corner(dy, dx)])
-
-
-BUFFERS, SEMAPHORES, GATHER_REFS = 8, 11, 8
+            sent(self.full.at[h.at(dy, 0), all_rows, : self.half], self.a_s.at[h.corner(dy, dx)])
+            sent(self.full.at[h.at(0, dx), all_rows, self.half :], self.b_s.at[h.corner(dy, dx)])
+
+
+BUFFERS, SEMAPHORES, GATHER_REFS, TOTAL_REFS = 8, 11, 8, 5
 
 
 def kernel(target_hbm, count_hbm, wave_hbm, precond_hbm, left_hbm, right_hbm, first_out, correction_out, second_out, *scratch):
@@ -305,14 +344,21 @@
 
     here = Place()
     buffers, more, sems = take(BUFFERS), take(BUFFERS), take(SEMAPHORES)
-    first, second = Exchange(here, buffers, sems), Exchange(here, more, sems)
+
+    def fold(x):
+        x = jnp.sum(x.reshape(x.shape[0] // 8, 8, width), axis=0)
+        return sum(x[:, c : c + 128] for c in range(0, width, 128))
+
+    def tally(r, part, value):
+        overlap.sums[0] += fold(wave[r, part] * value)
+
+    first, second = Exchange(here, buffers, sems, tally), Exchange(here, more, sems)
     wave, precond, image, left, right, r_high, r_low, v_high, v_low, in_high, in_low, target, count = take(13)
-    p_gather, f_gather = Gather(here, precond, take(GATHER_REFS), SLICES), Gather(here, image, take(GATHER_REFS), SLICES)
-    sums, mine, theirs, all_s, all_r, load = take(6)
-    terms, sectors, t, s = here.terms, here.sectors, here.t, here.s
+    p_gather, f_gather = Gather(here, precond, take(GATHER_REFS), EARLY), Gather(here, image, take(GATHER_REFS), SLICES)
+    overlap, share_total, (load,) = Total(here, take(TOTAL_REFS)), Total(here, take(TOTAL_REFS)), take(1)
+    t, s, terms = here.t, here.s, here.terms
     slots, _, rows, width = left.shape
     sub = rows // SLICES
-    peers = terms * sectors - 1
 
     order = here.corners + here.sides + here.own
     load_precond = pltpu.make_async_copy(precond_hbm, precond.at[t], load.at[0])
@@ -323,9 +369,9 @@
     load_left = [pltpu.make_async_copy(left_hbm.at[:, here.at(*o)], left.at[:, here.at(*o)], load.at[4 + slots + n])
                  for n, o in enumerate(order)]
     corners = len(here.corners)
-    arrived = barrier(here)
     for copy in [load_precond, load_wave, load_target, load_count] + load_left[:corners] + load_right + load_left[corners:]:
         copy.start()
+    arrived = barrier(here)
 
     def split_rows(value, start, size):
         for r in range(terms):
@@ -343,7 +389,8 @@
     def compute(exchange, slabs, part, size):
         high, low = inner(slabs, part)
         m = len(slabs) * size
-        tiles = [product(high[j * m : (j + 1) * m], low[j * m : (j + 1) * m], r_high[j], r_low[j]) for j in range(slots)]
+        outer = stacked if m < 128 else product
+        tiles = [outer(high[j * m : (j + 1) * m], low[j * m : (j + 1) * m], r_high[j], r_low[j]) for j in range(slots)]
         for n, o in enumerate(slabs):
             for p in range(3):
                 exchange.whole[p, here.at(*o), part] = sum(
@@ -378,123 +425,134 @@
                         ref = exchange.whole.at[p, here.at(*o)]
                         ref[...] = part if pair == pairs[0] else ref[...] + part
 
-    def apply(exchange, begin, finished, meanwhile):
+    def apply(exchange, begin, meanwhile):
         with jax.named_scope("CD"):
             begin()
         for i in range(SLICES):
             exchange.sectors_out(here.corners, i)
-        meanwhile(0)
-
-        @pl.loop(0, SLICES // 2)
+
+        @pl.loop(0, SLICES)
         def _(b):
             with jax.named_scope("C"):
-                compute(exchange, here.sides, pl.ds(pl.multiple_of(b * 2 * sub, 2 * sub), 2 * sub), 2 * sub)
-            exchange.sectors_out(here.sides, 2 * b)
-            exchange.sectors_out(here.sides, 2 * b + 1)
-            meanwhile(b + 1)
+                compute(exchange, here.sides, exchange.part(b), sub)
+            exchange.sectors_out(here.sides, b)
+            with jax.named_scope("p"):
+                meanwhile(b)
+
+            @pl.when(b >= 1)
+            def _():
+                with jax.named_scope("Fd"):
+                    exchange.corners(b - 1)
 
         with jax.named_scope("Fd"):
+            exchange.corners(SLICES - 1)
+
+        @pl.loop(0, 2)
+        def _(h):
+            with jax.named_scope("Fxy"):
+                exchange.sides(h)
+            with jax.named_scope("CO"):
+                size = rows // 2
+                compute(exchange, here.own, pl.ds(pl.multiple_of(h * size, size), size), size)
             for i in range(SLICES // 2):
-                exchange.corners(i)
-        with jax.named_scope("CO"):
-            compute(exchange, here.own, every, rows)
-        for i in range(SLICES):
-            exchange.sectors_out(here.own, i)
-        with jax.named_scope("Fd"):
-            for i in range(SLICES // 2, SLICES):
-                exchange.corners(i)
-        meanwhile(SLICES - 1)
-
-        @pl.loop(0, SLICES)
+                exchange.sectors_out(here.own, h * (SLICES // 2) + i)
+
+        @pl.loop(2, SLICES)
         def _(i):
             with jax.named_scope("Fxy"):
                 exchange.sides(i)
-
-        @pl.loop(0, SLICES)
-        def _(i):
-            with jax.named_scope("Fo"):
-                finished(i, exchange.own(i))
-
-    def fold(x):
-        x = jnp.sum(x.reshape(sub // 8, 8, width), axis=0)
-        return sum(x[:, c : c + 128] for c in range(0, width, 128))
 
     def first_begin():
         corners_first(first)
         for copy in load_left[corners:]:
             copy.wait()
 
-    def first_done(i, f):
+    def first_done(i):
         part = first.part(i)
+        f = first.own(i)
+        first_out[part] = f
         image[t, part] = f
-
-        @pl.when(i < SLICES - 1)
-        def _():
-            f_gather.begin(i)
-
-        first_out[part] = f
-        w, p = wave[t, part], precond[t, part]
-        wf, ww = w * f, w * w
-        for n, x in enumerate((wf, ww, wf * p, ww * p)):
-            sums[n] += fold(x)
 
     with jax.named_scope("enter"):
         load_precond.wait()
         arrived()
-        for i in range(SLICES):
+        for i in range(EARLY):
             p_gather.begin(i)
-    sums[...] = jnp.zeros_like(sums)
-    apply(first, first_begin, first_done, p_gather.relay)
-
-    def to_peer(k):
-        return send(mine, theirs.at[k - 1], all_s.at[0], all_r.at[0], **here.peer(k))
-
-    all_peers = send(theirs, theirs, all_s.at[0], all_r.at[0], **here.peer(1))
-    with jax.named_scope("sums"):
-        shape = (4, 128)
-        diagonal = lax.broadcasted_iota(jnp.int32, shape, 0) == lax.broadcasted_iota(jnp.int32, shape, 1)
-        line = jnp.sum(jnp.sum(sums[...], axis=1), axis=1, keepdims=True)
-        mine[...] = jnp.sum(jnp.where(diagonal, line, 0.0), axis=0, keepdims=True)
-
-        @pl.loop(1, peers + 1)
-        def _(k):
-            to_peer(k).start()
-
-    with jax.named_scope("relay2"):
-        f_gather.begin(SLICES - 1)
-        for i in range(SLICES):
+    overlap.sums[0] = jnp.zeros((8, 128), F32)
+    def relays(b):
+        @pl.when(b < EARLY)
+        def _():
+            p_gather.relay(b)
+
+    apply(first, first_begin, relays)
+
+    with jax.named_scope("Fo"):
+        for i in range(2):
+            first.merge(t, i)
+        first_done(0)
+        f_gather.begin(0)
+    with jax.named_scope("Mo"):
+        for i in range(2, SLICES):
+            first.merge(t, i)
+        overlap.sums[1] = fold(wave[t] * wave[t])
+        overlap.begin()
+    with jax.named_scope("Fo"):
+        for i in range(1, SLICES):
+            first_done(i)
+            if i < EARLY:
+                f_gather.begin(i)
+    with jax.named_scope("relay0"):
+        for i in range(EARLY):
             p_gather.finish(i)
-        for i in range(SLICES):
+        f_gather.relay(0)
+    with jax.named_scope("ray"):
+        cross, norm = overlap.finish()
+        rayleigh = cross / norm
+
+    def raw(r, part):
+        return precond[r, part] * (image[r, part] - rayleigh * wave[r, part])
+
+    with jax.named_scope("raw"):
+        share_total.sums[0] = jnp.zeros((8, 128), F32)
+        for i in reversed(range(SLICES)):
+            part = first.part(i)
+            own = raw(t, part)
+            correction_out[part] = own
+            share_total.sums[0] += fold(wave[t, part] * own)
+            if i >= EARLY:
+                image[t, part] = own
+        share_total.begin()
+        for i in range(EARLY, SLICES):
+            f_gather.begin(i)
+    with jax.named_scope("relay"):
+        for i in range(1, SLICES):
             f_gather.relay(i)
-    with jax.named_scope("peers"):
-        all_peers.wait_recv()
-
-    total = mine[...] + jnp.sum(theirs[...], axis=0)
-    cross, norm, a, b = (total[:, n : n + 1] for n in range(4))
-    rayleigh = cross / norm
-    share = (a - rayleigh * b) / norm
+    with jax.named_scope("share"):
+        (dot,) = share_total.finish()
+        share = dot / norm
+    correction_out[...] -= share * wave[t]
 
     def corrected(r, part):
-        return precond[r, part] * (image[r, part] - rayleigh * wave[r, part]) - share * wave[r, part]
-
-    correction_out[...] = corrected(t, every)
+        return raw(r, part) - share * wave[r, part]
+
     for i in range(SLICES):
         with jax.named_scope("gfin"):
             f_gather.finish(i)
         with jax.named_scope("corr"):
-            split_rows(corrected, i * sub, sub)
-
-    def second_done(i, total):
-        second_out[second.part(i)] = total
+            split_rows(corrected if i < EARLY else lambda r, part: image[r, part] - share * wave[r, part], i * sub, sub)
 
     first.drain()
-    apply(second, lambda: compute(second, here.corners, every, rows), second_done, lambda i: None)
+    apply(second, lambda: compute(second, here.corners, every, rows), lambda i: None)
+
+    @pl.loop(0, SLICES)
+    def _(i):
+        with jax.named_scope("Fo"):
+            second.merge(t, i)
+            second_out[second.part(i)] = second.own(i)
 
     with jax.named_scope("drain"):
-        second.drain()
-        p_gather.drain()
-        f_gather.drain()
-        all_peers.wait_send()
+        for stream in (second, p_gather, f_gather, overlap, share_total):
+            stream.drain()
 
 
 def publish_kernel(*refs):
@@ -527,9 +585,8 @@
         scratch_shapes=Exchange.buffers(width, terms) * 2 + Exchange.semaphores(terms)
         + [block, block, block, operators, pltpu.VMEM((slots, width, width), F32), halves, halves, half, half, inner, inner,
            pltpu.SMEM(out_sector.shape, jnp.int32), pltpu.SMEM(live_counts.shape, jnp.int32)]
-        + Gather.scratch(terms, SLICES) * 2
-        + [pltpu.VMEM((4, 8, 128), F32), pltpu.VMEM((1, 128), F32), pltpu.VMEM((peers, 1, 128), F32),
-           dma((1,)), dma((1,)), dma((4 + slots + terms,))],
+        + Gather.scratch(terms, EARLY) + Gather.scratch(terms, SLICES)
+        + Total.scratch(2, peers) + Total.scratch(1, peers) + [dma((4 + slots + terms,))],
         compiler_params=pltpu.CompilerParams(collective_id=0, has_side_effects=True, vmem_limit_bytes=VMEM_BYTES - 3 * 4 * rows * width - (192 << 10)),
     )(out_sector, live_counts, wavefunction.reshape(terms, rows, width), precond[0],
       left_ops.reshape(slots, terms, rows, width), right_ops[0])

time: 55.8 us -> 54.2 us (0.971)
  Pallas kernels: 54.4 us -> 52.7 us
    pallas_call x1, Pallas kernels: 53.5 us -> 51.8 us  [per_device(): pl.pallas_call(kernel, out_shape=(pltpu.VMEM((rows, width), F32),) * 3, i...]
where the time goes in v5:
time: 54.2 us; the launch traced here: 54 us
  Pallas kernels  52.7 us (97%)
  between operations  1.29 us (2%)
    pallas_call x1, Pallas kernels, per_device(): pl.pallas_call(kernel, out_shape=(pltpu.VMEM((rows, width), F32),) * 3, i...  51.8 us

profile of v5, /device:TPU:0, one launch (start us, length us, event | category | flops | bytes accessed | tf_op | source)
XLA Modules:
  0.0 54.0 jit_solution(9520396895505035212)
XLA Ops:
  1.3 51.8 %shard_map.85 = (f32[128,512]{1,0:T(8,128)S(1)}, f32[128,512]{1,0:T(8,128)S(1)}, f32[128,512]{1,0:T(8,128)S(1)}) custom-call(s32[1,4]{1,0:T(1,128)} %target_hbm.1, s32[1,1]{1,0:T(1,128)S(6)} %copy.9.count_hbm, f32[4,128,512]{2,1,0:T(8,128)} %bitcast.9, f32[128,512]{1,0:T(8,128)} %bitcast.10, f32[4,4,128,512]{3,2,1,0:T(8,128)} %bitcast.7, f32[4,512,512]{2,1,0:T(8,128)} %bitcast.8), custom_call_target="tpu_custom_call" | custom-call | tf_op jit(solution)/shard_map/pallas_call | solution.py:580
  53.1 0.9 %shard_map.86 = (f32[128,512]{1,0:T(8,128)}, f32[128,512]{1,0:T(8,128)}, f32[128,512]{1,0:T(8,128)}) custom-call(f32[128,512]{1,0:T(8,128)S(1)} %get-tuple-element.9.refs_0_, f32[128,512]{1,0:T(8,128)S(1)} %get-tuple-element.10.refs_1_, f32[128,512]{1,0:T(8,128)S(1)} %get-tuple-element.11.refs_2_), custom_call_target="tpu_custom_call" | custom-call | tf_op jit(solution)/shard_map/pallas_call | solution.py:593

commit v6 on v5

--- a/solution.py
+++ b/solution.py
@@ -386,11 +386,13 @@
         hit = jnp.logical_and(j < count[0, 0], target[0, j] - s + 1 == p)
         return jnp.where(hit, tile, 0.0)
 
+    def outer(m):
+        return stacked if m < 128 else product
+
     def compute(exchange, slabs, part, size):
         high, low = inner(slabs, part)
         m = len(slabs) * size
-        outer = stacked if m < 128 else product
-        tiles = [outer(high[j * m : (j + 1) * m], low[j * m : (j + 1) * m], r_high[j], r_low[j]) for j in range(slots)]
+        tiles = [outer(m)(high[j * m : (j + 1) * m], low[j * m : (j + 1) * m], r_high[j], r_low[j]) for j in range(slots)]
         for n, o in enumerate(slabs):
             for p in range(3):
                 exchange.whole[p, here.at(*o), part] = sum(
@@ -399,14 +401,15 @@
     every = pl.ds(0, rows)
 
     def corners_first(exchange):
-        m = corners * rows
+        part = pl.ds(0, rows // 2)
+        m = corners * (rows // 2)
         with jax.named_scope("startv"):
             load_wave.wait()
             split_rows(lambda r, part: wave[r, part], 0, rows)
         with jax.named_scope("startl"):
             for copy in load_left[:corners]:
                 copy.wait()
-            in_high[...], in_low[...] = inner(here.corners, every)
+            in_high[...], in_low[...] = inner(here.corners, part)
         load_target.wait()
         load_count.wait()
         pairs = [range(j, min(j + 2, slots)) for j in range(0, slots, 2)]
@@ -418,18 +421,33 @@
                 for j in pair:
                     high, low = split(right[j])
                     r_high[j], r_low[j] = high, low
-                    tiles[j] = product(in_high[j * m : (j + 1) * m], in_low[j * m : (j + 1) * m], high, low)
+                    tiles[j] = outer(m)(in_high[j * m : (j + 1) * m], in_low[j * m : (j + 1) * m], high, low)
                 for n, o in enumerate(here.corners):
                     for p in range(3):
-                        part = sum(chosen(j, p, tiles[j][n * rows : (n + 1) * rows]) for j in pair)
-                        ref = exchange.whole.at[p, here.at(*o)]
-                        ref[...] = part if pair == pairs[0] else ref[...] + part
+                        rows_of = slice(n * (rows // 2), (n + 1) * (rows // 2))
+                        piece = sum(chosen(j, p, tiles[j][rows_of]) for j in pair)
+                        ref = exchange.whole.at[p, here.at(*o), part]
+                        ref[...] = piece if pair == pairs[0] else ref[...] + piece
 
     def apply(exchange, begin, meanwhile):
-        with jax.named_scope("CD"):
+        def half(h):
+            return pl.ds(pl.multiple_of(h * (rows // 2), rows // 2), rows // 2)
+
+        def half_out(slabs, h):
+            for i in range(SLICES // 2):
+                exchange.sectors_out(slabs, h * (SLICES // 2) + i)
+
+        def corner_block(h):
+            with jax.named_scope("CD"):
+                compute(exchange, here.corners, half(h), rows // 2)
+            half_out(here.corners, h)
+
+        if begin:
             begin()
-        for i in range(SLICES):
-            exchange.sectors_out(here.corners, i)
+            half_out(here.corners, 0)
+            corner_block(1)
+        else:
+            pl.loop(0, 2)(corner_block)
 
         @pl.loop(0, SLICES)
         def _(b):
@@ -439,23 +457,22 @@
             with jax.named_scope("p"):
                 meanwhile(b)
 
-            @pl.when(b >= 1)
-            def _():
-                with jax.named_scope("Fd"):
-                    exchange.corners(b - 1)
-
-        with jax.named_scope("Fd"):
-            exchange.corners(SLICES - 1)
+            with jax.named_scope("Fd"):
+                @pl.when(b < SLICES - 1)
+                def _():
+                    exchange.corners(b + b // 2)
+
+                @pl.when(b == 1)
+                def _():
+                    exchange.corners(2)
 
         @pl.loop(0, 2)
         def _(h):
             with jax.named_scope("Fxy"):
                 exchange.sides(h)
             with jax.named_scope("CO"):
-                size = rows // 2
-                compute(exchange, here.own, pl.ds(pl.multiple_of(h * size, size), size), size)
-            for i in range(SLICES // 2):
-                exchange.sectors_out(here.own, h * (SLICES // 2) + i)
+                compute(exchange, here.own, half(h), rows // 2)
+            half_out(here.own, h)
 
         @pl.loop(2, SLICES)
         def _(i):
@@ -513,17 +530,16 @@
         return precond[r, part] * (image[r, part] - rayleigh * wave[r, part])
 
     with jax.named_scope("raw"):
+        for i in range(EARLY, SLICES):
+            image[t, first.part(i)] = raw(t, first.part(i))
+            f_gather.begin(i)
         share_total.sums[0] = jnp.zeros((8, 128), F32)
-        for i in reversed(range(SLICES)):
+        for i in range(SLICES):
             part = first.part(i)
-            own = raw(t, part)
+            own = raw(t, part) if i < EARLY else image[t, part]
             correction_out[part] = own
             share_total.sums[0] += fold(wave[t, part] * own)
-            if i >= EARLY:
-                image[t, part] = own
         share_total.begin()
-        for i in range(EARLY, SLICES):
-            f_gather.begin(i)
     with jax.named_scope("relay"):
         for i in range(1, SLICES):
             f_gather.relay(i)
@@ -542,7 +558,7 @@
             split_rows(corrected if i < EARLY else lambda r, part: image[r, part] - share * wave[r, part], i * sub, sub)
 
     first.drain()
-    apply(second, lambda: compute(second, here.corners, every, rows), lambda i: None)
+    apply(second, None, lambda i: None)
 
     @pl.loop(0, SLICES)
     def _(i):
@@ -575,7 +591,7 @@
     half = pltpu.VMEM((width, width), BF16)
     operators = pltpu.VMEM((slots, terms, rows, width), F32)
     halves = pltpu.VMEM((slots, width, width), BF16)
-    inner = pltpu.VMEM((slots * (gy - 1) * (gx - 1) * rows, width), BF16)
+    inner = pltpu.VMEM((slots * (gy - 1) * (gx - 1) * (rows // 2), width), BF16)
     peers = terms * sectors - 1
     outs = pl.pallas_call(
         kernel,

time: 54.2 us -> 53.5 us (0.987)
  Pallas kernels: 52.7 us -> 52 us
    pallas_call x1, Pallas kernels: 51.8 us -> 51.1 us  [per_device(): pl.pallas_call(kernel, out_shape=(pltpu.VMEM((rows, width), F32),) * 3, i...]
where the time goes in v6:
time: 53.5 us; the launch traced here: 53.3 us
  Pallas kernels  52 us (97%)
  between operations  1.29 us (2%)
    pallas_call x1, Pallas kernels, per_device(): pl.pallas_call(kernel, out_shape=(pltpu.VMEM((rows, width), F32),) * 3, i...  51.1 us

profile of v6, /device:TPU:0, one launch (start us, length us, event | category | flops | bytes accessed | tf_op | source)
XLA Modules:
  0.0 53.3 jit_solution(9993138250102377470)
XLA Ops:
  1.3 51.1 %shard_map.85 = (f32[128,512]{1,0:T(8,128)S(1)}, f32[128,512]{1,0:T(8,128)S(1)}, f32[128,512]{1,0:T(8,128)S(1)}) custom-call(s32[1,4]{1,0:T(1,128)} %target_hbm.1, s32[1,1]{1,0:T(1,128)S(6)} %copy.9.count_hbm, f32[4,128,512]{2,1,0:T(8,128)} %bitcast.9, f32[128,512]{1,0:T(8,128)} %bitcast.10, f32[4,4,128,512]{3,2,1,0:T(8,128)} %bitcast.7, f32[4,512,512]{2,1,0:T(8,128)} %bitcast.8), custom_call_target="tpu_custom_call" | custom-call | tf_op jit(solution)/shard_map/pallas_call | solution.py:596
  52.4 0.9 %shard_map.86 = (f32[128,512]{1,0:T(8,128)}, f32[128,512]{1,0:T(8,128)}, f32[128,512]{1,0:T(8,128)}) custom-call(f32[128,512]{1,0:T(8,128)S(1)} %get-tuple-element.9.refs_0_, f32[128,512]{1,0:T(8,128)S(1)} %get-tuple-element.10.refs_1_, f32[128,512]{1,0:T(8,128)S(1)} %get-tuple-element.11.refs_2_), custom_call_target="tpu_custom_call" | custom-call | tf_op jit(solution)/shard_map/pallas_call | solution.py:609

commit v7 on v6

--- a/solution.py
+++ b/solution.py
@@ -259,7 +259,7 @@
 class Gather:
     def __init__(self, here, full, refs, pieces):
         self.here, self.full = here, full
-        self.x_s, self.x_r, self.y_s, self.y_r, self.a_s, self.a_r, self.b_s, self.b_r = refs
+        self.x_s, self.x_r, self.y_s, self.y_r, self.a_s, self.a_r, self.b_s, self.b_r, self.c_s, self.c_r = refs
         self.sub, self.half, self.pieces = full.shape[1] // SLICES, full.shape[2] // 2, pieces
 
     @staticmethod
@@ -268,7 +268,7 @@
         dma = pltpu.SemaphoreType.DMA
         corners = (gy - 1) * (gx - 1)
         return [dma((gx - 1,)), dma((pieces, gx - 1)), dma((gy - 1,)), dma((pieces, gy - 1))] + [
-            dma((corners,)), dma((pieces, corners))] * 2
+            dma((corners,)), dma((pieces, corners))] * 2 + [dma((corners,)), dma((corners,))]
 
     def part(self, i):
         return pl.ds(pl.multiple_of(i * self.sub, self.sub), self.sub)
@@ -288,6 +288,28 @@
     def relay_b(self, r, dy, dx, i):
         ref, c = self.full.at[r, self.part(i), self.half :], self.here.corner(dy, dx)
         return send(ref, ref, self.b_s.at[c], self.b_r.at[i, c], term=self.here.at(dy, 0))
+
+    def to_corner(self, r, dy, dx, i):
+        ref, c = self.full.at[r, self.part(i)], self.here.corner(dy, dx)
+        return send(ref, ref, self.c_s.at[c], self.c_r.at[c], term=self.here.at(dy, dx))
+
+    def begin_direct(self, i):
+        for dy, dx in self.here.corners:
+            self.to_corner(self.here.t, dy, dx, i).start()
+        self.begin(i)
+
+    def finish_direct(self, i):
+        h = self.here
+        for dx in range(1, h.gx):
+            self.to_x(h.at(0, dx), h.gx - dx, i).wait_recv()
+        for dy in range(1, h.gy):
+            self.to_y(h.at(dy, 0), h.gy - dy, i).wait_recv()
+        for dy, dx in h.corners:
+            self.to_corner(h.at(h.gy - dy, h.gx - dx), dy, dx, i).wait_recv()
+
+    def drain_direct(self, i):
+        for dy, dx in self.here.corners:
+            self.to_corner(self.here.t, dy, dx, i).wait_send()
 
     def begin(self, i):
         h = self.here
@@ -318,6 +340,7 @@
 
     def drain(self):
         h, all_rows = self.here, pl.ds(0, self.pieces * self.sub)
+        relayed = pl.ds(0, EARLY * self.sub)
 
         def sent(ref, sem):
             send(ref, ref, sem, self.x_r.at[0, 0], term=h.at(0, 1)).wait_send()
@@ -327,11 +350,11 @@
         for n in range(h.gy - 1):
             sent(self.full.at[h.t, all_rows], self.y_s.at[n])
         for dy, dx in h.corners:
-            sent(self.full.at[h.at(dy, 0), all_rows, : self.half], self.a_s.at[h.corner(dy, dx)])
-            sent(self.full.at[h.at(0, dx), all_rows, self.half :], self.b_s.at[h.corner(dy, dx)])
-
-
-BUFFERS, SEMAPHORES, GATHER_REFS, TOTAL_REFS = 8, 11, 8, 5
+            sent(self.full.at[h.at(dy, 0), relayed, : self.half], self.a_s.at[h.corner(dy, dx)])
+            sent(self.full.at[h.at(0, dx), relayed, self.half :], self.b_s.at[h.corner(dy, dx)])
+
+
+BUFFERS, SEMAPHORES, GATHER_REFS, TOTAL_REFS = 8, 11, 10, 5
 
 
 def kernel(target_hbm, count_hbm, wave_hbm, precond_hbm, left_hbm, right_hbm, first_out, correction_out, second_out, *scratch):
@@ -445,26 +468,38 @@
         if begin:
             begin()
             half_out(here.corners, 0)
+            for i in range(EARLY):
+                p_gather.begin(i)
             corner_block(1)
         else:
             pl.loop(0, 2)(corner_block)
 
-        @pl.loop(0, SLICES)
-        def _(b):
-            with jax.named_scope("C"):
-                compute(exchange, here.sides, exchange.part(b), sub)
-            exchange.sectors_out(here.sides, b)
-            with jax.named_scope("p"):
-                meanwhile(b)
-
-            with jax.named_scope("Fd"):
-                @pl.when(b < SLICES - 1)
-                def _():
-                    exchange.corners(b + b // 2)
-
-                @pl.when(b == 1)
-                def _():
-                    exchange.corners(2)
+        if begin:
+            @pl.loop(0, SLICES)
+            def _(b):
+                with jax.named_scope("C"):
+                    compute(exchange, here.sides, exchange.part(b), sub)
+                exchange.sectors_out(here.sides, b)
+                with jax.named_scope("p"):
+                    meanwhile(b)
+
+                with jax.named_scope("Fd"):
+                    @pl.when(b < SLICES - 1)
+                    def _():
+                        exchange.corners(b + b // 2)
+
+                    @pl.when(b == 1)
+                    def _():
+                        exchange.corners(2)
+        else:
+            @pl.loop(0, 2)
+            def _(h):
+                with jax.named_scope("C"):
+                    compute(exchange, here.sides, half(h), rows // 2)
+                half_out(here.sides, h)
+                with jax.named_scope("Fd"):
+                    for i in range(SLICES // 2):
+                        exchange.corners(h * (SLICES // 2) + i)
 
         @pl.loop(0, 2)
         def _(h):
@@ -481,6 +516,9 @@
 
     def first_begin():
         corners_first(first)
+        with jax.named_scope("enter"):
+            load_precond.wait()
+            arrived()
         for copy in load_left[corners:]:
             copy.wait()
 
@@ -490,16 +528,11 @@
         first_out[part] = f
         image[t, part] = f
 
-    with jax.named_scope("enter"):
-        load_precond.wait()
-        arrived()
-        for i in range(EARLY):
-            p_gather.begin(i)
     overlap.sums[0] = jnp.zeros((8, 128), F32)
     def relays(b):
-        @pl.when(b < EARLY)
+        @pl.when(jnp.logical_and(b >= 1, b <= EARLY))
         def _():
-            p_gather.relay(b)
+            p_gather.relay(b - 1)
 
     apply(first, first_begin, relays)
 
@@ -532,7 +565,6 @@
     with jax.named_scope("raw"):
         for i in range(EARLY, SLICES):
             image[t, first.part(i)] = raw(t, first.part(i))
-            f_gather.begin(i)
         share_total.sums[0] = jnp.zeros((8, 128), F32)
         for i in range(SLICES):
             part = first.part(i)
@@ -540,8 +572,10 @@
             correction_out[part] = own
             share_total.sums[0] += fold(wave[t, part] * own)
         share_total.begin()
+        for i in range(EARLY, SLICES):
+            f_gather.begin_direct(i)
     with jax.named_scope("relay"):
-        for i in range(1, SLICES):
+        for i in range(1, EARLY):
             f_gather.relay(i)
     with jax.named_scope("share"):
         (dot,) = share_total.finish()
@@ -553,7 +587,10 @@
 
     for i in range(SLICES):
         with jax.named_scope("gfin"):
-            f_gather.finish(i)
+            if i < EARLY:
+                f_gather.finish(i)
+            else:
+                f_gather.finish_direct(i)
         with jax.named_scope("corr"):
             split_rows(corrected if i < EARLY else lambda r, part: image[r, part] - share * wave[r, part], i * sub, sub)
 
@@ -569,6 +606,7 @@
     with jax.named_scope("drain"):
         for stream in (second, p_gather, f_gather, overlap, share_total):
             stream.drain()
+        f_gather.drain_direct(EARLY)
 
 
 def publish_kernel(*refs):

time: 53.5 us -> 52.3 us (0.978)
  Pallas kernels: 52 us -> 50.8 us
    pallas_call x1, Pallas kernels: 51.1 us -> 49.9 us  [per_device(): pl.pallas_call(kernel, out_shape=(pltpu.VMEM((rows, width), F32),) * 3, i...]
where the time goes in v7:
time: 52.3 us; the launch traced here: 52.1 us
  Pallas kernels  50.8 us (97%)
  between operations  1.29 us (2%)
    pallas_call x1, Pallas kernels, per_device(): pl.pallas_call(kernel, out_shape=(pltpu.VMEM((rows, width), F32),) * 3, i...  49.9 us

profile of v7, /device:TPU:0, one launch (start us, length us, event | category | flops | bytes accessed | tf_op | source)
XLA Modules:
  0.0 52.1 jit_solution(6836795620391896712)
XLA Ops:
  1.3 49.9 %shard_map.85 = (f32[128,512]{1,0:T(8,128)S(1)}, f32[128,512]{1,0:T(8,128)S(1)}, f32[128,512]{1,0:T(8,128)S(1)}) custom-call(s32[1,4]{1,0:T(1,128)} %target_hbm.1, s32[1,1]{1,0:T(1,128)S(6)} %copy.9.count_hbm, f32[4,128,512]{2,1,0:T(8,128)} %bitcast.9, f32[128,512]{1,0:T(8,128)} %bitcast.10, f32[4,4,128,512]{3,2,1,0:T(8,128)} %bitcast.7, f32[4,512,512]{2,1,0:T(8,128)} %bitcast.8), custom_call_target="tpu_custom_call" | custom-call | tf_op jit(solution)/shard_map/pallas_call | solution.py:634
  51.2 0.9 %shard_map.86 = (f32[128,512]{1,0:T(8,128)}, f32[128,512]{1,0:T(8,128)}, f32[128,512]{1,0:T(8,128)}) custom-call(f32[128,512]{1,0:T(8,128)S(1)} %get-tuple-element.9.refs_0_, f32[128,512]{1,0:T(8,128)S(1)} %get-tuple-element.10.refs_1_, f32[128,512]{1,0:T(8,128)S(1)} %get-tuple-element.11.refs_2_), custom_call_target="tpu_custom_call" | custom-call | tf_op jit(solution)/shard_map/pallas_call | solution.py:647

commit v8 on v7

--- a/solution.py
+++ b/solution.py
@@ -383,16 +383,21 @@
     slots, _, rows, width = left.shape
     sub = rows // SLICES
 
-    order = here.corners + here.sides + here.own
     load_precond = pltpu.make_async_copy(precond_hbm, precond.at[t], load.at[0])
     load_wave = pltpu.make_async_copy(wave_hbm, wave, load.at[1])
     load_target = pltpu.make_async_copy(target_hbm, target, load.at[2])
     load_count = pltpu.make_async_copy(count_hbm, count, load.at[3])
     load_right = [pltpu.make_async_copy(right_hbm.at[j], right.at[j], load.at[4 + j]) for j in range(slots)]
-    load_left = [pltpu.make_async_copy(left_hbm.at[:, here.at(*o)], left.at[:, here.at(*o)], load.at[4 + slots + n])
-                 for n, o in enumerate(order)]
+    def load_rows(o, part, n):
+        piece = (slice(None), here.at(*o), part)
+        return pltpu.make_async_copy(left_hbm.at[piece], left.at[piece], load.at[4 + slots + n])
+
+    upper, lower = pl.ds(0, rows // 2), pl.ds(rows // 2, rows // 2)
+    load_soon = [load_rows(o, upper, n) for n, o in enumerate(here.corners)]
+    load_later = [load_rows(o, lower, terms + n) for n, o in enumerate(here.corners)] + [
+        load_rows(o, pl.ds(0, rows), len(here.corners) + n) for n, o in enumerate(here.sides + here.own)]
     corners = len(here.corners)
-    for copy in [load_precond, load_wave, load_target, load_count] + load_left[:corners] + load_right + load_left[corners:]:
+    for copy in [load_wave] + load_soon + [load_target, load_count] + load_right + [load_precond] + load_later:
         copy.start()
     arrived = barrier(here)
 
@@ -430,7 +435,7 @@
             load_wave.wait()
             split_rows(lambda r, part: wave[r, part], 0, rows)
         with jax.named_scope("startl"):
-            for copy in load_left[:corners]:
+            for copy in load_soon:
                 copy.wait()
             in_high[...], in_low[...] = inner(here.corners, part)
         load_target.wait()
@@ -470,6 +475,8 @@
             half_out(here.corners, 0)
             for i in range(EARLY):
                 p_gather.begin(i)
+            for copy in load_later:
+                copy.wait()
             corner_block(1)
         else:
             pl.loop(0, 2)(corner_block)
@@ -492,14 +499,24 @@
                     def _():
                         exchange.corners(2)
         else:
-            @pl.loop(0, 2)
-            def _(h):
+            with jax.named_scope("C"):
+                compute(exchange, here.sides, half(0), rows // 2)
+            half_out(here.sides, 0)
+            with jax.named_scope("Fd"):
+                for i in range(SLICES // 2):
+                    exchange.corners(i)
+
+            @pl.loop(SLICES // 2, SLICES)
+            def _(i):
                 with jax.named_scope("C"):
-                    compute(exchange, here.sides, half(h), rows // 2)
-                half_out(here.sides, h)
-                with jax.named_scope("Fd"):
-                    for i in range(SLICES // 2):
-                        exchange.corners(h * (SLICES // 2) + i)
+                    compute(exchange, here.sides, exchange.part(i), sub)
+                exchange.sectors_out(here.sides, i)
+
+                @pl.when(i == SLICES // 2)
+                def _():
+                    with jax.named_scope("Fd"):
+                        for k in range(SLICES // 2, SLICES):
+                            exchange.corners(k)
 
         @pl.loop(0, 2)
         def _(h):
@@ -519,8 +536,6 @@
         with jax.named_scope("enter"):
             load_precond.wait()
             arrived()
-        for copy in load_left[corners:]:
-            copy.wait()
 
     def first_done(i):
         part = first.part(i)
@@ -640,7 +655,7 @@
         + [block, block, block, operators, pltpu.VMEM((slots, width, width), F32), halves, halves, half, half, inner, inner,
            pltpu.SMEM(out_sector.shape, jnp.int32), pltpu.SMEM(live_counts.shape, jnp.int32)]
         + Gather.scratch(terms, EARLY) + Gather.scratch(terms, SLICES)
-        + Total.scratch(2, peers) + Total.scratch(1, peers) + [dma((4 + slots + terms,))],
+        + Total.scratch(2, peers) + Total.scratch(1, peers) + [dma((4 + slots + terms + (gy - 1) * (gx - 1),))],
         compiler_params=pltpu.CompilerParams(collective_id=0, has_side_effects=True, vmem_limit_bytes=VMEM_BYTES - 3 * 4 * rows * width - (192 << 10)),
     )(out_sector, live_counts, wavefunction.reshape(terms, rows, width), precond[0],
       left_ops.reshape(slots, terms, rows, width), right_ops[0])

time: 52.3 us -> 52.6 us (level)
  no operation moved by 1% of the time
where the time goes in v8:
time: 52.6 us; the launch traced here: 52.5 us
  Pallas kernels  51.2 us (97%)
  between operations  1.29 us (2%)
    pallas_call x1, Pallas kernels, per_device(): pl.pallas_call(kernel, out_shape=(pltpu.VMEM((rows, width), F32),) * 3, i...  50.3 us

profile of v8, /device:TPU:0, one launch (start us, length us, event | category | flops | bytes accessed | tf_op | source)
XLA Modules:
  0.0 52.5 jit_solution(16127184857082833051)
XLA Ops:
  1.3 50.3 %shard_map.85 = (f32[128,512]{1,0:T(8,128)S(1)}, f32[128,512]{1,0:T(8,128)S(1)}, f32[128,512]{1,0:T(8,128)S(1)}) custom-call(s32[1,4]{1,0:T(1,128)} %target_hbm.1, s32[1,1]{1,0:T(1,128)S(6)} %copy.9.count_hbm, f32[4,128,512]{2,1,0:T(8,128)} %bitcast.9, f32[128,512]{1,0:T(8,128)} %bitcast.10, f32[4,4,128,512]{3,2,1,0:T(8,128)} %bitcast.7, f32[4,512,512]{2,1,0:T(8,128)} %bitcast.8), custom_call_target="tpu_custom_call" | custom-call | tf_op jit(solution)/shard_map/pallas_call | solution.py:649
  51.6 0.9 %shard_map.86 = (f32[128,512]{1,0:T(8,128)}, f32[128,512]{1,0:T(8,128)}, f32[128,512]{1,0:T(8,128)}) custom-call(f32[128,512]{1,0:T(8,128)S(1)} %get-tuple-element.9.refs_0_, f32[128,512]{1,0:T(8,128)S(1)} %get-tuple-element.10.refs_1_, f32[128,512]{1,0:T(8,128)S(1)} %get-tuple-element.11.refs_2_), custom_call_target="tpu_custom_call" | custom-call | tf_op jit(solution)/shard_map/pallas_call | solution.py:662

commit v9 on v8

--- a/solution.py
+++ b/solution.py
@@ -397,7 +397,7 @@
     load_later = [load_rows(o, lower, terms + n) for n, o in enumerate(here.corners)] + [
         load_rows(o, pl.ds(0, rows), len(here.corners) + n) for n, o in enumerate(here.sides + here.own)]
     corners = len(here.corners)
-    for copy in [load_wave] + load_soon + [load_target, load_count] + load_right + [load_precond] + load_later:
+    for copy in [load_wave] + load_soon + [load_target, load_count, load_precond] + load_right + load_later:
         copy.start()
     arrived = barrier(here)
 
@@ -456,6 +456,12 @@
                         piece = sum(chosen(j, p, tiles[j][rows_of]) for j in pair)
                         ref = exchange.whole.at[p, here.at(*o), part]
                         ref[...] = piece if pair == pairs[0] else ref[...] + piece
+            if pair == pairs[0]:
+                with jax.named_scope("enter"):
+                    load_precond.wait()
+                    arrived()
+                    for i in range(EARLY):
+                        p_gather.begin(i)
 
     def apply(exchange, begin, meanwhile):
         def half(h):
@@ -473,8 +479,6 @@
         if begin:
             begin()
             half_out(here.corners, 0)
-            for i in range(EARLY):
-                p_gather.begin(i)
             for copy in load_later:
                 copy.wait()
             corner_block(1)
@@ -533,9 +537,6 @@
 
     def first_begin():
         corners_first(first)
-        with jax.named_scope("enter"):
-            load_precond.wait()
-            arrived()
 
     def first_done(i):
         part = first.part(i)

time: 52.6 us -> 52.6 us (level)
  no operation moved by 1% of the time
where the time goes in v9:
time: 52.6 us; the launch traced here: 52.5 us
  Pallas kernels  51.2 us (97%)
  between operations  1.29 us (2%)
    pallas_call x1, Pallas kernels, per_device(): pl.pallas_call(kernel, out_shape=(pltpu.VMEM((rows, width), F32),) * 3, i...  50.3 us

profile of v9, /device:TPU:0, one launch (start us, length us, event | category | flops | bytes accessed | tf_op | source)
XLA Modules:
  0.0 52.5 jit_solution(9531547358387820935)
XLA Ops:
  1.3 50.3 %shard_map.85 = (f32[128,512]{1,0:T(8,128)S(1)}, f32[128,512]{1,0:T(8,128)S(1)}, f32[128,512]{1,0:T(8,128)S(1)}) custom-call(s32[1,4]{1,0:T(1,128)} %target_hbm.1, s32[1,1]{1,0:T(1,128)S(6)} %copy.9.count_hbm, f32[4,128,512]{2,1,0:T(8,128)} %bitcast.9, f32[128,512]{1,0:T(8,128)} %bitcast.10, f32[4,4,128,512]{3,2,1,0:T(8,128)} %bitcast.7, f32[4,512,512]{2,1,0:T(8,128)} %bitcast.8), custom_call_target="tpu_custom_call" | custom-call | tf_op jit(solution)/shard_map/pallas_call | solution.py:650
  51.5 0.9 %shard_map.86 = (f32[128,512]{1,0:T(8,128)}, f32[128,512]{1,0:T(8,128)}, f32[128,512]{1,0:T(8,128)}) custom-call(f32[128,512]{1,0:T(8,128)S(1)} %get-tuple-element.9.refs_0_, f32[128,512]{1,0:T(8,128)S(1)} %get-tuple-element.10.refs_1_, f32[128,512]{1,0:T(8,128)S(1)} %get-tuple-element.11.refs_2_), custom_call_target="tpu_custom_call" | custom-call | tf_op jit(solution)/shard_map/pallas_call | solution.py:663

commit v10 on v7

--- a/solution.py
+++ b/solution.py
@@ -474,32 +474,16 @@
         else:
             pl.loop(0, 2)(corner_block)
 
-        if begin:
-            @pl.loop(0, SLICES)
-            def _(b):
-                with jax.named_scope("C"):
-                    compute(exchange, here.sides, exchange.part(b), sub)
-                exchange.sectors_out(here.sides, b)
-                with jax.named_scope("p"):
-                    meanwhile(b)
-
-                with jax.named_scope("Fd"):
-                    @pl.when(b < SLICES - 1)
-                    def _():
-                        exchange.corners(b + b // 2)
-
-                    @pl.when(b == 1)
-                    def _():
-                        exchange.corners(2)
-        else:
-            @pl.loop(0, 2)
-            def _(h):
-                with jax.named_scope("C"):
-                    compute(exchange, here.sides, half(h), rows // 2)
-                half_out(here.sides, h)
-                with jax.named_scope("Fd"):
-                    for i in range(SLICES // 2):
-                        exchange.corners(h * (SLICES // 2) + i)
+        @pl.loop(0, 2)
+        def _(h):
+            with jax.named_scope("C"):
+                compute(exchange, here.sides, half(h), rows // 2)
+            half_out(here.sides, h)
+            with jax.named_scope("Fd"):
+                for i in range(SLICES // 2):
+                    exchange.corners(h * (SLICES // 2) + i)
+            with jax.named_scope("p"):
+                meanwhile(h)
 
         @pl.loop(0, 2)
         def _(h):
@@ -529,10 +513,11 @@
         image[t, part] = f
 
     overlap.sums[0] = jnp.zeros((8, 128), F32)
-    def relays(b):
-        @pl.when(jnp.logical_and(b >= 1, b <= EARLY))
-        def _():
-            p_gather.relay(b - 1)
+    def relays(h):
+        for i in range(EARLY):
+            @pl.when(h == (i + 1) // 2)
+            def _():
+                p_gather.relay(i)
 
     apply(first, first_begin, relays)
 

time: 52.3 us -> 52.3 us (level)
  no operation moved by 1% of the time
where the time goes in v10:
time: 52.3 us; the launch traced here: 52.1 us
  Pallas kernels  50.9 us (97%)
  between operations  1.29 us (2%)
    pallas_call x1, Pallas kernels, per_device(): pl.pallas_call(kernel, out_shape=(pltpu.VMEM((rows, width), F32),) * 3, i...  49.9 us

profile of v10, /device:TPU:0, one launch (start us, length us, event | category | flops | bytes accessed | tf_op | source)
XLA Modules:
  0.0 52.1 jit_solution(7626620016137110874)
XLA Ops:
  1.3 49.9 %shard_map.85 = (f32[128,512]{1,0:T(8,128)S(1)}, f32[128,512]{1,0:T(8,128)S(1)}, f32[128,512]{1,0:T(8,128)S(1)}) custom-call(s32[1,4]{1,0:T(1,128)} %target_hbm.1, s32[1,1]{1,0:T(1,128)S(6)} %copy.9.count_hbm, f32[4,128,512]{2,1,0:T(8,128)} %bitcast.9, f32[128,512]{1,0:T(8,128)} %bitcast.10, f32[4,4,128,512]{3,2,1,0:T(8,128)} %bitcast.7, f32[4,512,512]{2,1,0:T(8,128)} %bitcast.8), custom_call_target="tpu_custom_call" | custom-call | tf_op jit(solution)/shard_map/pallas_call | solution.py:619
  51.2 0.9 %shard_map.86 = (f32[128,512]{1,0:T(8,128)}, f32[128,512]{1,0:T(8,128)}, f32[128,512]{1,0:T(8,128)}) custom-call(f32[128,512]{1,0:T(8,128)S(1)} %get-tuple-element.9.refs_0_, f32[128,512]{1,0:T(8,128)S(1)} %get-tuple-element.10.refs_1_, f32[128,512]{1,0:T(8,128)S(1)} %get-tuple-element.11.refs_2_), custom_call_target="tpu_custom_call" | custom-call | tf_op jit(solution)/shard_map/pallas_call | solution.py:632
